TPU v7x, 32 devices: a whole 2x2x4 slice. The times are simulated.
32 devices in a mesh: dp: 8 (over z, y), tensor: 4 (over x, core).
Axes of the slice: x: 2, y: 2, z: 4, core: 2. Of those that a mesh axis runs over, the one named last changes fastest.
Arguments:
- activations: bfloat16 [4096, 6144], P('dp', 'tensor'), may hold values from -6 to 6
- cotangent: bfloat16 [4096, 5120], P('dp'), may hold values from -0.09375 to 0.09375
- master: float32 [5120, 6144], P('dp', 'tensor'), may hold values from -0.078125 to 0.078125
- moment_one: float32 [5120, 6144], P('dp', 'tensor'), may hold values from -0.3 to 0.3
- moment_two: float32 [5120, 6144], P('dp', 'tensor'), may hold values from 0.0002 to 0.002
- prompts: bfloat16 [1536, 6144], P('dp', 'tensor'), may hold values from -6 to 6
Outputs:
- new_master: float32 [5120, 6144], P('dp', 'tensor')
- new_moment_one: float32 [5120, 6144], P('dp', 'tensor')
- new_moment_two: float32 [5120, 6144], P('dp', 'tensor')
- projected: bfloat16 [1536, 5120], P(('dp', 'tensor'))
All inputs are finite; a program needn't handle non-finite values.
Results may differ from a plain program's by a relative error of at most 0.03.
Values may be sent and summed in bfloat16 or wider, within the bound.
No kernel may reach another device: no remote copies, remote signals or barrier semaphores. Data moves between devices by JAX's collectives and lax.ppermute only.
A program may use at most 128 MiB of HBM per device.

v0:
```python
import jax
import jax.numpy as jnp
from jax import lax
from jax.sharding import PartitionSpec as P


def local(activations, cotangent, master, moment_one, moment_two, prompts):
    columns = cotangent
    grad = lax.psum_scatter(
        lax.dot_general(
            columns, activations, (((0,), (0,)), ((), ())), preferred_element_type=jnp.float32
        ).astype(jnp.bfloat16),
        "dp",
        scatter_dimension=0,
        tiled=True,
    ).astype(jnp.float32)
    new_one = 0.9 * moment_one + 0.1 * grad
    new_two = 0.999 * moment_two + 0.001 * grad * grad
    first = new_one / (1.0 - 0.9**50)
    second = new_two / (1.0 - 0.999**50)
    new_master = master - 0.003 * (first / (jnp.sqrt(second) + 1e-08) + 0.01 * master)
    rollout_weight = new_master.astype(jnp.bfloat16)
    partial_out = lax.dot_general(
        lax.all_gather(prompts, "dp", axis=0, tiled=True),
        rollout_weight,
        (((1,), (1,)), ((), ())),
        preferred_element_type=jnp.float32,
    )
    groups = lax.axis_size("dp")
    shares = lax.axis_size("tensor")
    owned = prompts.shape[0] // shares
    columns = rollout_weight.shape[0]
    grouped = partial_out.reshape(groups, shares, owned, columns).transpose(1, 0, 2, 3)
    grouped = grouped.reshape(shares * groups * owned, columns)
    summed = lax.psum_scatter(
        grouped.astype(jnp.bfloat16), "tensor", scatter_dimension=0, tiled=True
    )
    summed = summed.reshape(groups, owned, columns)
    joined = lax.all_to_all(summed, "dp", split_axis=0, concat_axis=2, tiled=True)
    projected = joined.reshape(owned, groups * columns)
    return (new_master, new_one, new_two, projected)


def solution(mesh):
    placed = (
        P("dp", "tensor"),
        P("dp", None),
        P("dp", "tensor"),
        P("dp", "tensor"),
        P("dp", "tensor"),
        P("dp", "tensor"),
    )
    return jax.shard_map(
        local,
        mesh=mesh,
        in_specs=placed,
        out_specs=(
            P("dp", "tensor"),
            P("dp", "tensor"),
            P("dp", "tensor"),
            P(("dp", "tensor"), None),
        ),
        check_vma=False,
    )
```

profile of v0, /device:TPU:0, one launch (start us, length us, event | category | flops | bytes accessed | tf_op | source)
XLA Modules:
  0.0 424.9 jit_solution(10129300150587916178)
XLA Ops:
  7.2 0.0 copy-start
  7.2 0.0 reduce-scatter.3.cloned.1.call-start
  7.2 1.4 copy-done
  8.6 13.7 %convolution_convert_fusion = bf16[5120,1536]{1,0:T(8,128)(2,1)} fusion(bf16[512,5120]{1,0:T(8,128)(2,1)} %param.7, bf16[512,1536]{1,0:T(8,128)(2,1)S(1)} %copy-done), kind=kOutput, calls=%fused_computation | convolution fusion | flops 8060928000 | bytes 22544384 | tf_op jit(solution)/shard_map/dot_general | solution.py:10
  22.3 0.0 reduce-scatter.3.cloned.1.call-update
  22.4 0.0 all-gather.2.cloned.1.call-start
  22.4 0.7 all-gather.2.cloned.1.call-update
  23.1 0.0 reduce-scatter.5.cloned.1.call-start
  23.2 253.4 %reduce-scatter.3.cloned.1.call-done = bf16[640,1536]{1,0:T(8,128)(2,1)} async-done(((bf16[5120,1536]{1,0:T(8,128)(2,1)}), bf16[640,1536]{1,0:T(8,128)(2,1)}) %reduce-scatter.3.cloned.1.call-update) | async-done | bytes 1966096 | tf_op jit(solution)/shard_map/reduce_scatter | solution.py:9
  276.5 9.3 %multiply_subtract_fusion = (f32[640,1536]{1,0:T(8,128)}, f32[640,1536]{1,0:T(8,128)}, f32[640,1536]{1,0:T(8,128)}) fusion(f32[640,1536]{1,0:T(8,128)} %param.8, bf16[640,1536]{1,0:T(8,128)(2,1)} %reduce-scatter.3.cloned.1.call-done, f32[640,1536]{1,0:T(8,128)} %param.9, f32[640,1536]{1,0:T(8,128)} %param.10), kind=kLoop, calls=%fused_computation.5 | loop fusion | flops 15728640 | bytes 25559040 | tf_op jit(solution)/shard_map/sub | solution.py:21
  285.8 71.4 %all-gather.2.cloned.1.call-done = bf16[1536,1536]{1,0:T(8,128)(2,1)} async-done(((bf16[192,1536]{1,0:T(8,128)(2,1)}), bf16[1536,1536]{1,0:T(8,128)(2,1)}) %all-gather.2.cloned.1.call-update) | async-done | bytes 4718608 | tf_op jit(solution)/shard_map/all_gather | solution.py:24
  357.2 8.1 %fusion.2 = bf16[1536,640]{0,1:T(8,128)(2,1)} fusion(bf16[1536,1536]{1,0:T(8,128)(2,1)} %all-gather.2.cloned.1.call-done, f32[640,1536]{1,0:T(8,128)} %get-tuple-element.4), kind=kOutput, calls=%fused_computation.7 | convolution fusion | flops 3021864960 | bytes 10616832 | tf_op jit(solution)/shard_map/dot_general | solution.py:23
  365.2 2.8 copy.12
  368.0 1.5 copy.13
  369.5 0.0 reduce-scatter.5.cloned.1.call-update
  369.5 28.9 %reduce-scatter.5.cloned.1.call-done = bf16[384,640]{1,0:T(8,128)(2,1)} async-done(((bf16[1536,640]{1,0:T(8,128)(2,1)}), bf16[384,640]{1,0:T(8,128)(2,1)}) %reduce-scatter.5.cloned.1.call-update) | async-done | bytes 491536 | tf_op jit(solution)/shard_map/reduce_scatter | solution.py:35
  398.4 19.2 %all_to_all.15 = bf16[8,48,640]{2,1,0:T(8,128)(2,1)S(1)} all-to-all(bf16[8,48,640]{2,1,0:T(8,128)(2,1)} %bitcast.22), channel_id=1, replica_groups=mesh['dp'=8,'tensor'=4] {'dp'}, dimensions={0} | all-to-all | bytes 983040 | tf_op jit(solution)/shard_map/all_to_all | solution.py:39
  417.6 0.8 copy.15
Async XLA Ops:
  7.2 1.4 copy-start
  7.2 269.4 %reduce-scatter.3.cloned.1.call-start = ((), (), s32[]{:S(2)}) async-start(), calls=%async_computation.3 | async-start | bytes 17694720 | tf_op jit(solution)/shard_map/reduce_scatter | solution.py:9
  22.4 334.8 %all-gather.2.cloned.1.call-start = ((), (), s32[]{:S(2)}) async-start(), calls=%async_computation.4 | async-start | bytes 5308416 | tf_op jit(solution)/shard_map/all_gather | solution.py:24
  23.1 375.3 %reduce-scatter.5.cloned.1.call-start = ((), (), s32[]{:S(2)}) async-start(), calls=%async_computation.5 | async-start | bytes 2457600 | tf_op jit(solution)/shard_map/reduce_scatter | solution.py:35
Sparse Core Ops, SparseCore 0:
  22.5 254.0 reduce-scatter.2
  278.7 78.3 all-gather.1
  369.6 28.7 reduce-scatter.4
where the time goes:
time: 425 us
  waiting for transfers between devices  354 us (83%)
  matrix products  21.8 us (5%)
  blocking collectives  19.2 us (5%)
  between operations  13.8 us (3%)
  other arithmetic  9.25 us (2%)
  local copies, waits for them, and re-layouts  6.44 us (2%)
    reduce_scatter x1, waiting for transfers between devices, local(): lax.psum_scatter(lax.dot_general(columns, activations, (((0,), (0,)), (()...  253 us
    all_gather x1, waiting for transfers between devices, local(): lax.all_gather(prompts, 'dp', axis=0, tiled=True)  71.4 us
    reduce_scatter x1, waiting for transfers between devices, local(): lax.psum_scatter(grouped.astype(jnp.bfloat16), 'tensor', scatter_dimensio...  28.9 us
    all_to_all x1, blocking collectives, local(): lax.all_to_all(summed, 'dp', split_axis=0, concat_axis=2, tiled=True)  19.2 us
    dot_general x1, matrix products, local(): lax.dot_general(columns, activations, (((0,), (0,)), ((), ())), preferred...  13.7 us
    sub x1, other arithmetic, local(): master - 0.003 * (first / (jnp.sqrt(second) + 1e-08) + 0.01 * master)  9.25 us
  transfers between devices with their start and end apart: 3, of which 3 were waited for; matrix products, arithmetic and copies ran while one was open for 2% of the time, Pallas kernels for 0%

commit v1 on v0

v1 whole, which is shorter than its diff:
```python
import functools
import math

import jax
import jax.numpy as jnp
from jax import lax
from jax.experimental import pallas as pl
from jax.experimental.pallas import tpu as pltpu
from jax.sharding import PartitionSpec as P


GROUP = 4
SHARE = 4
COLUMN_PARTS = 2
TILE = 128


def swap(x, axis, bit):
    n = lax.axis_size(axis)
    return lax.ppermute(x, axis, [(i, i ^ bit) for i in range(n)])


def dot_tokens(cot, acts):
    return lax.dot_general(cot, acts, (((0,), (0,)), ((), ())), preferred_element_type=jnp.float32)


def dot_features(rows, weight):
    return lax.dot_general(rows, weight, (((1,), (1,)), ((), ())), preferred_element_type=jnp.float32)


def row_parts(rows):
    if rows % 128:
        return [(0, rows)]
    first = (rows // 128 * 3 + 4) // 5 * 128
    return [(0, first), (first, rows - first)] if first < rows else [(0, rows)]


def adam_kernel(n_recv, *refs):
    own, recvs = refs[0], refs[1 : 1 + n_recv]
    master, one, two = refs[1 + n_recv : 4 + n_recv]
    new_master, new_one, new_two, weight = refs[-4:]
    grad = own[...]
    for recv in recvs:
        grad = grad + recv[...].astype(jnp.float32)
    first = 0.9 * one[...] + 0.1 * grad
    second = 0.999 * two[...] + 0.001 * grad * grad
    new_one[...] = first
    new_two[...] = second
    held = master[...]
    step = (first * (1.0 / (1.0 - 0.9**50))) / (jnp.sqrt(second * (1.0 / (1.0 - 0.999**50))) + 1e-08)
    updated = held - 0.003 * (step + 0.01 * held)
    new_master[...] = updated
    weight[...] = updated.astype(jnp.bfloat16)


def adam(own, recvs, state, previous, row, column):
    rows, width = recvs[0].shape if recvs else own.shape
    full = state[0].shape
    tile = math.gcd(math.gcd(rows, row), TILE) if rows % TILE == 0 else rows
    here = pl.BlockSpec((tile, width), lambda i: (i, 0))
    below = pl.BlockSpec((tile, width), lambda i: (i + row // tile, 0))
    there = pl.BlockSpec((tile, width), lambda i: (i + row // tile, column // width))
    held = list(previous) if previous is not None else []
    n_in = 1 + len(recvs) + 3
    return pl.pallas_call(
        functools.partial(adam_kernel, len(recvs)),
        grid=(rows // tile,),
        in_specs=[below] + [here] * len(recvs) + [there] * 3 + [pl.BlockSpec(memory_space=pl.ANY)] * len(held),
        out_specs=[there] * 3 + [here],
        out_shape=[jax.ShapeDtypeStruct(full, jnp.float32)] * 3 + [jax.ShapeDtypeStruct((rows, width), jnp.bfloat16)],
        input_output_aliases={n_in + j: j for j in range(len(held))},
        cost_estimate=pl.CostEstimate(flops=20 * rows * width, bytes_accessed=32 * rows * width, transcendentals=2 * rows * width),
        name="adam",
    )(own, *recvs, *state, *held)


def place_kernel(rows, starts, me, *refs):
    out = refs[-1]
    for start, blocks in zip(starts, refs):
        n, _, size = blocks.shape
        for p in range(n):
            out[:, p * rows + start : p * rows + start + size] = blocks[lax.bitwise_xor(me[0], p)]


def gate(x, after):
    return lax.optimization_barrier((x, after))[0]


def send_cotangent(cotangent, tokens, rows, me, share, order):
    k, m = me // GROUP, me % GROUP
    part = tokens // SHARE
    got = {}
    for s in (3, 2, 1):
        pieces = [
            lax.dynamic_slice(cotangent, (share * part, ((k ^ c) * GROUP + (m ^ s)) * rows), (part, rows)) for c in order
        ]
        got[s] = swap(jnp.concatenate(pieces, axis=1), "dp", s)
    return got


def join_shares(mine, across, both, share, rows):
    peers, part, width = mine.shape
    whole = jnp.zeros((peers, SHARE * part, width), mine.dtype)
    for offset, piece in ((0, mine), (2, across), (1, both[0]), (3, both[1])):
        whole = lax.dynamic_update_slice(whole, piece, (0, (share ^ offset) * part, 0))
    return [[whole[s, :, i : i + rows] for s in range(peers)] for i in range(0, width, rows)]


def reduce_over_tensor(accs, n, owned, t, marks):
    n_tensor, size = lax.axis_size("tensor"), accs[0].shape[1]
    if n_tensor & (n_tensor - 1):
        acc = jnp.concatenate(accs)
        grouped = acc.reshape(n, n_tensor, owned, size).transpose(1, 0, 2, 3).astype(jnp.bfloat16)
        return lax.psum_scatter(grouped, "tensor", scatter_dimension=0, tiled=True).reshape(n, owned, size)
    lefts, bit = [acc.reshape(-1, n_tensor, owned, size) for acc in accs], 1
    while bit < n_tensor:
        mine = (t // bit) % 2
        pairs = [left.reshape(left.shape[0], left.shape[1] // 2, 2, owned, size) for left in lefts]
        going = [lax.dynamic_index_in_dim(pair, 1 - mine, 2, keepdims=False).astype(jnp.bfloat16) for pair in pairs]
        going = jnp.concatenate(going)
        marks.append(going)
        came = swap(going, "tensor", bit).astype(jnp.float32)
        lefts, at = [], 0
        for pair in pairs:
            kept = lax.dynamic_index_in_dim(pair, mine, 2, keepdims=False)
            lefts.append(kept + came[at : at + kept.shape[0]])
            at += kept.shape[0]
        bit *= 2
    return jnp.concatenate([left.reshape(-1, owned, size).astype(jnp.bfloat16) for left in lefts])


def exchange_over_dp(blocks, seen, n):
    blocks = {q: blocks[i] for i, q in enumerate(seen)}
    bit = n // 2
    while bit:
        going = [q for q in range(n) if q & bit]
        came = swap(jnp.stack([blocks[q] for q in going]), "dp", bit)
        blocks.update({q: came[i] for i, q in enumerate(going)})
        bit //= 2
    return jnp.stack([blocks[q] for q in range(n)])


def local(activations, cotangent, master, moment_one, moment_two, prompts):
    n, n_tensor = lax.axis_size("dp"), lax.axis_size("tensor")
    me, t = lax.axis_index("dp"), lax.axis_index("tensor")
    k, m = me // GROUP, me % GROUP
    n_groups = n // GROUP
    tokens, width = activations.shape
    rows = master.shape[0]
    state = (master, moment_one, moment_two)
    part_width = width // COLUMN_PARTS
    order = [*range(1, n_groups), 0]

    share = t % SHARE
    away = order[:-1]
    got = send_cotangent(cotangent, tokens, rows, me, share, order)

    blocks = [activations[:, j * part_width : (j + 1) * part_width] for j in range(COLUMN_PARTS)]
    ahead = [swap(block, "dp", 1) for block in blocks]
    side = [swap(block, "dp", 2) for block in blocks]
    diagonal = [swap(beside, "dp", 1) for beside in side]

    mine_of = {
        tag: jnp.stack([got[s][:, low:high] for s in (1, 2, 3)])
        for tag, low, high in (("a", 0, len(away) * rows), ("h", len(away) * rows, len(order) * rows))
    }
    across_of = {tag: swap(mine, "tensor", 2) for tag, mine in mine_of.items()}

    def cotangents(tag, across):
        both = swap(jnp.stack([mine_of[tag], across]), "tensor", 1)
        return join_shares(mine_of[tag], across, both, share, rows)

    def group_sum(j, c, cots, after):
        own = lax.dynamic_slice(cotangent, (0, ((k ^ c) * GROUP + m) * rows), (tokens, rows))
        if after is not None:
            own = gate(own, after)
        acc = dot_tokens(own, blocks[j])
        firsts[j] = acc
        acc = acc + dot_tokens(cots[0], ahead[j]) + dot_tokens(cots[1], side[j])
        return acc + dot_tokens(cots[2], gate(diagonal[j], acc))

    firsts = {}
    last = COLUMN_PARTS - 1
    parts = row_parts(rows)
    cots_away = cotangents("a", across_of["a"])
    sent = [group_sum(0, c, cots_away[i], None).astype(jnp.bfloat16) for i, c in enumerate(away)]
    received = {(0, 0): [swap(x, "dp", c * GROUP) for x, c in zip(sent, away)]}
    mark, early_mark = sent[-1], firsts[0]

    cots_home = cotangents("h", gate(across_of["h"], mark))
    own_sums = [group_sum(0, 0, cots_home[0], mark)]
    for j in range(1, COLUMN_PARTS):
        sums = [group_sum(j, c, cots_away[i], mark) for i, c in enumerate(away)]
        for start, size in parts if j == last else [(0, rows)]:
            sent = [x[start : start + size].astype(jnp.bfloat16) for x in sums]
            received[j, start] = [swap(x, "dp", c * GROUP) for x, c in zip(sent, away)]
        mark = sent[-1]
        own_sums.append(group_sum(j, 0, cots_home[0], mark))

    seen, held, bit = [0], [prompts], n // 2
    while bit > 1:
        held.append(swap(jnp.concatenate(held) if len(held) > 1 else held[0], "dp", bit))
        if bit > 2:
            held[-1] = gate(held[-1], early_mark)
        seen += [q ^ bit for q in seen]
        bit //= 2
    near = jnp.concatenate(held[:-1])
    far = held[-1]

    near_other = swap(near, "dp", 1)
    new_state, weights = None, []
    for j in range(last):
        recvs = [gate(x, mark) for x in received[j, 0]]
        *new_state, weight = adam(own_sums[j], recvs, state, new_state, 0, j * part_width)
        weights.append(weight)
    far = gate(far, mark)
    far_other = swap(far, "dp", 1)
    seen += [q ^ 1 for q in seen]

    def early_part(some):
        return [dot_features(some[:, j * part_width : (j + 1) * part_width], weights[j]) for j in range(last)]

    def late_part(some, done, weight, start, size):
        return sum((e[:, start : start + size] for e in done), start=dot_features(some[:, last * part_width :], weight))

    most = jnp.concatenate([near, far, near_other])
    early = early_part(most)
    early_other, mark = None, early[-1]
    owned = prompts.shape[0] // n_tensor
    outs = []
    for start, size in parts:
        recvs = [gate(x, mark) for x in received[last, start]]
        *new_state, weight = adam(own_sums[last], recvs, state, new_state, start, last * part_width)
        acc = late_part(most, early, weight, start, size)
        if early_other is None:
            far_other = gate(far_other, acc)
            early_other = early_part(far_other)
        acc_other = late_part(far_other, early_other, weight, start, size)
        marks = []
        left = reduce_over_tensor([acc, acc_other], n, owned, t, marks)
        mark = marks[0] if marks else acc_other
        outs.append(exchange_over_dp(left, seen, n))
    projected = pl.pallas_call(
        functools.partial(place_kernel, rows, [start for start, _ in parts]),
        in_specs=[pl.BlockSpec(memory_space=pltpu.SMEM)] + [pl.BlockSpec(memory_space=pltpu.VMEM)] * len(outs),
        out_specs=pl.BlockSpec(memory_space=pltpu.VMEM),
        out_shape=jax.ShapeDtypeStruct((owned, n * rows), jnp.bfloat16),
        name="place",
    )(me.reshape(1), *outs)
    return (*new_state, projected)


def solution(mesh):
    placed = (
        P("dp", "tensor"),
        P("dp", None),
        P("dp", "tensor"),
        P("dp", "tensor"),
        P("dp", "tensor"),
        P("dp", "tensor"),
    )
    return jax.shard_map(
        local,
        mesh=mesh,
        in_specs=placed,
        out_specs=(
            P("dp", "tensor"),
            P("dp", "tensor"),
            P("dp", "tensor"),
            P(("dp", "tensor"), None),
        ),
        check_vma=False,
    )
```

time: 425 us -> 257 us (0.60)
  waiting for transfers between devices: 354 us -> 128 us
  starting transfers between devices: 0.12 us -> 34.6 us
  matrix products: 21.8 us -> 44.2 us
  blocking collectives: 19.2 us -> 0 us
  Pallas kernels: 0 us -> 18.4 us
  local copies, waits for them, and re-layouts: 6.44 us -> 21.6 us
  between operations: 13.8 us -> 1.47 us
    reduce_scatter x2 -> x0, waiting for transfers between devices: 282 us -> none  [the longest x1 253 us: local(): lax.psum_scatter(lax.dot_general(columns, activations, (((0,), (0,)), (()...]
    ppermute x0 -> x30, waiting for transfers between devices: none -> 128 us  [swap(): return lax.ppermute(x, axis, [(i, i ^ bit) for i in range(n)])]
    all_gather x1 -> x0, waiting for transfers between devices: 71.4 us -> none  [local(): lax.all_gather(prompts, 'dp', axis=0, tiled=True)]
    ppermute x0 -> x30, starting transfers between devices: none -> 34.6 us  [swap(): return lax.ppermute(x, axis, [(i, i ^ bit) for i in range(n)])]
    dot_general x2 -> x22, matrix products: 21.8 us -> 44.2 us  [the longest x16 27.9 us: dot_tokens(): lax.dot_general(cot, acts, (((0,), (0,)), ((), ())), preferred_element_ty...]
    all_to_all x1 -> x0, blocking collectives: 19.2 us -> none  [local(): lax.all_to_all(summed, 'dp', split_axis=0, concat_axis=2, tiled=True)]
    pallas_call x0 -> x4, Pallas kernels: none -> 18.4 us  [the longest x3 16.6 us: adam(): pl.pallas_call(functools.partial(adam_kernel, len(recvs)), grid=(rows //...]
    sub x1 -> x0, other arithmetic: 9.25 us -> none  [local(): master - 0.003 * (first / (jnp.sqrt(second) + 1e-08) + 0.01 * master)]
  transfers between devices with their start and end apart: 3 -> 30, of which waited for: 3 -> 15; matrix products, arithmetic and copies ran while one was open for 2% -> 24% of each run, Pallas kernels for 0% -> 5%
where the time goes in v1:
time: 257 us; the launch traced here: 256 us
  waiting for transfers between devices  128 us (50%)
  matrix products  44.2 us (17%)
  starting transfers between devices  34.6 us (13%)
  local copies, waits for them, and re-layouts  21.6 us (8%)
  Pallas kernels  18.4 us (7%)
  other arithmetic  7.89 us (3%)
    ppermute x30, waiting for transfers between devices, swap(): return lax.ppermute(x, axis, [(i, i ^ bit) for i in range(n)])  128 us
    ppermute x30, starting transfers between devices, swap(): return lax.ppermute(x, axis, [(i, i ^ bit) for i in range(n)])  34.6 us
    dot_general x16, matrix products, dot_tokens(): lax.dot_general(cot, acts, (((0,), (0,)), ((), ())), preferred_element_ty...  27.9 us
    pallas_call x3, Pallas kernels, adam(): pl.pallas_call(functools.partial(adam_kernel, len(recvs)), grid=(rows //...  16.6 us
    dot_general x6, matrix products, dot_features(): lax.dot_general(rows, weight, (((1,), (1,)), ((), ())), preferred_element...  16.3 us
  transfers between devices with their start and end apart: 30, of which 15 were waited for; matrix products, arithmetic and copies ran while one was open for 24% of the time, Pallas kernels for 5%

profile of v1, /device:TPU:0, one launch (start us, length us, event | category | flops | bytes accessed | tf_op | source)
XLA Modules:
  0.0 256.2 jit_solution(658015904365916101)
XLA Ops:
  2.2 4.1 %collective-permute-start.2 = (bf16[128,1280]{1,0:T(8,128)(2,1)S(1)}, bf16[128,1280]{1,0:T(8,128)(2,1)S(1)}, u32[]{:S(2)}, u32[]{:S(2)}) collective-permute-start(bf16[128,1280]{1,0:T(8,128)(2,1)S(1)} %pad_maximum_fusion.8), channel_id=1, source_target_pairs={{0,12},{4,8},{8,4},{12,0},{16,28},{20,24},{24,20},{28,16},{1,13},{... | collective-permute-start | bytes 983048 | tf_op jit(solution)/shard_map/ppermute | solution.py:20
  7.0 7.8 %collective-permute-done.2 = bf16[128,1280]{1,0:T(8,128)(2,1)S(1)} collective-permute-done((bf16[128,1280]{1,0:T(8,128)(2,1)S(1)}, bf16[128,1280]{1,0:T(8,128)(2,1)S(1)}, u32[]{:S(2)}, u32[]{:S(2)}) %collective-permute-start.2) | collective-permute-done | bytes 327712 | tf_op jit(solution)/shard_map/ppermute | solution.py:20
  15.5 5.6 %collective-permute-done.1 = bf16[128,1280]{1,0:T(8,128)(2,1)S(1)} collective-permute-done((bf16[128,1280]{1,0:T(8,128)(2,1)S(1)}, bf16[128,1280]{1,0:T(8,128)(2,1)S(1)}, u32[]{:S(2)}, u32[]{:S(2)}) %collective-permute-start.1) | collective-permute-done | bytes 327712 | tf_op jit(solution)/shard_map/ppermute | solution.py:20
  42.8 18.0 %collective-permute-done.14 = bf16[192,1536]{1,0:T(8,128)(2,1)} collective-permute-done((bf16[192,1536]{1,0:T(8,128)(2,1)}, bf16[192,1536]{1,0:T(8,128)(2,1)}, u32[]{:S(2)}, u32[]{:S(2)}) %collective-permute-start.14) | collective-permute-done | bytes 589856 | tf_op jit(solution)/shard_map/ppermute | solution.py:20
  64.1 12.9 %collective-permute-done.6 = bf16[512,768]{1,0:T(8,128)(2,1)} collective-permute-done((bf16[512,768]{1,0:T(8,128)(2,1)}, bf16[512,768]{1,0:T(8,128)(2,1)}, u32[]{:S(2)}, u32[]{:S(2)}) %collective-permute-start.6) | collective-permute-done | bytes 786464 | tf_op jit(solution)/shard_map/ppermute | solution.py:20
  89.0 9.2 %collective-permute-done.7 = bf16[512,768]{1,0:T(8,128)(2,1)S(1)} collective-permute-done((bf16[512,768]{1,0:T(8,128)(2,1)}, bf16[512,768]{1,0:T(8,128)(2,1)S(1)}, u32[]{:S(2)}, u32[]{:S(2)}) %collective-permute-start.7) | collective-permute-done | bytes 786464 | tf_op jit(solution)/shard_map/ppermute | solution.py:20
  101.2 2.7 %collective-permute-start.18 = (bf16[640,768]{1,0:T(8,128)(2,1)S(1)}, bf16[640,768]{1,0:T(8,128)(2,1)S(1)}, u32[]{:S(2)}, u32[]{:S(2)}) collective-permute-start(bf16[640,768]{1,0:T(8,128)(2,1)S(1)} %add_convert_fusion.1), channel_id=1, source_target_pairs={{0,16},{4,20},{8,24},{12,28},{16,0},{20,4},{24,8},{28,12},{1,17},{... | collective-permute-start | bytes 2949128 | tf_op jit(solution)/shard_map/ppermute | solution.py:20
  108.0 29.7 %collective-permute-done.10 = bf16[512,768]{1,0:T(8,128)(2,1)S(1)} collective-permute-done((bf16[512,768]{1,0:T(8,128)(2,1)}, bf16[512,768]{1,0:T(8,128)(2,1)S(1)}, u32[]{:S(2)}, u32[]{:S(2)}) %collective-permute-start.10) | collective-permute-done | bytes 786464 | tf_op jit(solution)/shard_map/ppermute | solution.py:20
  141.5 2.6 %collective-permute-start.13 = (bf16[256,768]{1,0:T(8,128)(2,1)}, bf16[256,768]{1,0:T(8,128)(2,1)}, u32[]{:S(2)}, u32[]{:S(2)}) collective-permute-start(bf16[256,768]{1,0:T(8,128)(2,1)} %slice.376), channel_id=1, source_target_pairs={{0,16},{4,20},{8,24},{12,28},{16,0},{20,4},{24,8},{28,12},{1,17},{... | collective-permute-start | bytes 1179656 | tf_op jit(solution)/shard_map/ppermute | solution.py:20
  153.5 3.4 %add_add_fusion.1 = f32[640,768]{1,0:T(8,128)} fusion(f32[640,768]{1,0:T(8,128)S(1)} %fusion.24, f32[640,768]{1,0:T(8,128)S(1)} %fusion.9, bf16[512,768]{1,0:T(8,128)(2,1)} %collective-permute-done.9, bf16[3,512,640]{2,1,0:T(8,128)(2,1)S(1)} %fusion.12), kind=kOutput, calls=%fused_computation.3 | convolution fusion | flops 504299520 | bytes 7340032 | tf_op jit(solution)/shard_map/dot_general | solution.py:24
  158.9 8.0 %adam.3 = (f32[640,1536]{1,0:T(8,128)}, f32[640,1536]{1,0:T(8,128)}, f32[640,1536]{1,0:T(8,128)}, bf16[640,768]{1,0:T(8,128)(2,1)}) custom-call(f32[640,768]{1,0:T(8,128)} %convolution_add_fusion.2.refs_0_, bf16[640,768]{1,0:T(8,128)(2,1)} %copy-done.16, f32[640,1536]{1,0:T(8,128)} %refs_2_.5, f32[640,1536]{1,0:T(8,128)} %refs_3_.5, f32[640,1536]{1,0:T(8,128)} %refs_4_.5), custom_call_target="tpu_custom_call" | custom-call | flops 9830400 | bytes 15728640 | tf_op jit(solution)/shard_map/adam/pallas_call | solution.py:65
  166.9 5.1 %fusion = f32[1152,640]{1,0:T(8,128)} fusion(bf16[640,768]{1,0:T(8,128)(2,1)} %get-tuple-element.41, bf16[1152,1536]{1,0:T(8,128)(2,1)} %copy-done.6), kind=kOutput, calls=%fused_computation.8 | convolution fusion | flops 1132462080 | bytes 5701632 | tf_op jit(solution)/shard_map/dot_general | solution.py:28
  172.0 12.8 %collective-permute-done.17.refs_1_ = bf16[384,768]{1,0:T(8,128)(2,1)} collective-permute-done((bf16[384,768]{1,0:T(8,128)(2,1)}, bf16[384,768]{1,0:T(8,128)(2,1)}, u32[]{:S(2)}, u32[]{:S(2)}) %collective-permute-start.17) | collective-permute-done | bytes 589856 | tf_op jit(solution)/shard_map/ppermute | solution.py:20
  186.9 5.4 %adam.4 = (f32[640,1536]{1,0:T(8,128)}, f32[640,1536]{1,0:T(8,128)}, f32[640,1536]{1,0:T(8,128)}, bf16[384,768]{1,0:T(8,128)(2,1)}) custom-call(f32[640,768]{1,0:T(8,128)} %convolution_add_fusion.3.refs_0_, bf16[384,768]{1,0:T(8,128)(2,1)} %collective-permute-done.17.refs_1_, ...), custom_call_target="tpu_custom_call", output_to_operand_aliasing={{0}: (5, {}), {1}: (6, {}), {2}: (7, {})} | custom-call | flops 5898240 | bytes 9437184 | tf_op jit(solution)/shard_map/adam/pallas_call | solution.py:65
  192.3 3.4 %convolution_add_fusion = f32[1152,384]{1,0:T(8,128)S(1)} fusion(bf16[384,768]{1,0:T(8,128)(2,1)} %get-tuple-element.46, f32[1152,640]{1,0:T(8,128)} %fusion, bf16[1152,1536]{1,0:T(8,128)(2,1)} %copy-done.6), kind=kOutput, calls=%fused_computation | convolution fusion | flops 679919616 | bytes 5898240 | tf_op jit(solution)/shard_map/dot_general | solution.py:28
  200.1 3.3 %adam.5 = (f32[640,1536]{1,0:T(8,128)}, f32[640,1536]{1,0:T(8,128)}, f32[640,1536]{1,0:T(8,128)}, bf16[256,768]{1,0:T(8,128)(2,1)}) custom-call(f32[640,768]{1,0:T(8,128)} %convolution_add_fusion.3.refs_0_, bf16[256,768]{1,0:T(8,128)(2,1)} %collective-permute-done.13.refs_1_, ...), custom_call_target="tpu_custom_call", output_to_operand_aliasing={{0}: (5, {}), {1}: (6, {}), {2}: (7, {})} | custom-call | flops 3932160 | bytes 6291456 | tf_op jit(solution)/shard_map/adam/pallas_call | solution.py:65
  203.4 2.6 %convolution_add_fusion.1 = f32[1152,256]{1,0:T(8,128)S(1)} fusion(bf16[256,768]{1,0:T(8,128)(2,1)} %get-tuple-element.55, bf16[1152,1536]{1,0:T(8,128)(2,1)} %copy-done.6, f32[1152,640]{1,0:T(8,128)} %fusion), kind=kOutput, calls=%fused_computation.1 | convolution fusion | flops 453279744 | bytes 4521984 | tf_op jit(solution)/shard_map/dot_general | solution.py:28
  215.6 5.1 %collective-permute-done.26 = bf16[8,1,48,256]{3,2,1,0:T(8,128)(2,1)S(1)} collective-permute-done((bf16[8,1,48,256]{3,2,1,0:T(8,128)(2,1)S(1)}, bf16[8,1,48,256]{3,2,1,0:T(8,128)(2,1)S(1)}, u32[]{:S(2)}, u32[]{:S(2)}) %collective-permute-start.26) | collective-permute-done | bytes 196640 | tf_op jit(solution)/shard_map/ppermute | solution.py:20
  222.6 5.4 %collective-permute-done.27 = bf16[4,48,256]{2,1,0:T(8,128)(2,1)S(1)} collective-permute-done((bf16[4,48,256]{2,1,0:T(8,128)(2,1)S(1)}, bf16[4,48,256]{2,1,0:T(8,128)(2,1)S(1)}, u32[]{:S(2)}, u32[]{:S(2)}) %collective-permute-start.27) | collective-permute-done | bytes 98336 | tf_op jit(solution)/shard_map/ppermute | solution.py:20
  228.0 4.6 %collective-permute-done.28 = bf16[4,48,256]{2,1,0:T(8,128)(2,1)S(1)} collective-permute-done((bf16[4,48,256]{2,1,0:T(8,128)(2,1)S(1)}, bf16[4,48,256]{2,1,0:T(8,128)(2,1)S(1)}, u32[]{:S(2)}, u32[]{:S(2)}) %collective-permute-start.28) | collective-permute-done | bytes 98336 | tf_op jit(solution)/shard_map/ppermute | solution.py:20
  235.2 3.0 %collective-permute-start.22 = (bf16[4,48,384]{2,1,0:T(8,128)(2,1)S(1)}, bf16[4,48,384]{2,1,0:T(8,128)(2,1)S(1)}, u32[]{:S(2)}, u32[]{:S(2)}) collective-permute-start(bf16[4,48,384]{2,1,0:T(8,128)(2,1)S(1)} %pad_maximum_fusion.11), channel_id=1, source_target_pairs={{0,16},{4,20},{8,24},{12,28},{16,0},{20,4},{24,8},{28,12},{1,17},{... | collective-permute-start | bytes 442376 | tf_op jit(solution)/shard_map/ppermute | solution.py:20
  238.2 4.8 %collective-permute-done.22 = bf16[4,48,384]{2,1,0:T(8,128)(2,1)S(1)} collective-permute-done((bf16[4,48,384]{2,1,0:T(8,128)(2,1)S(1)}, bf16[4,48,384]{2,1,0:T(8,128)(2,1)S(1)}, u32[]{:S(2)}, u32[]{:S(2)}) %collective-permute-start.22) | collective-permute-done | bytes 147488 | tf_op jit(solution)/shard_map/ppermute | solution.py:20
  244.0 4.2 %collective-permute-done.23 = bf16[4,48,384]{2,1,0:T(8,128)(2,1)S(1)} collective-permute-done((bf16[4,48,384]{2,1,0:T(8,128)(2,1)S(1)}, bf16[4,48,384]{2,1,0:T(8,128)(2,1)S(1)}, u32[]{:S(2)}, u32[]{:S(2)}) %collective-permute-start.23) | collective-permute-done | bytes 147488 | tf_op jit(solution)/shard_map/ppermute | solution.py:20
  249.2 4.3 %collective-permute-done.24 = bf16[4,48,384]{2,1,0:T(8,128)(2,1)S(1)} collective-permute-done((bf16[4,48,384]{2,1,0:T(8,128)(2,1)S(1)}, bf16[4,48,384]{2,1,0:T(8,128)(2,1)S(1)}, u32[]{:S(2)}, u32[]{:S(2)}) %collective-permute-start.24) | collective-permute-done | bytes 147488 | tf_op jit(solution)/shard_map/ppermute | solution.py:20
  (183 shorter events, 86.7 us)
Async XLA Ops:
  2.2 12.7 %collective-permute-start.2 = (bf16[128,1280]{1,0:T(8,128)(2,1)S(1)}, bf16[128,1280]{1,0:T(8,128)(2,1)S(1)}, u32[]{:S(2)}, u32[]{:S(2)}) collective-permute-start(bf16[128,1280]{1,0:T(8,128)(2,1)S(1)} %pad_maximum_fusion.8), channel_id=1, source_target_pairs={{0,12},{4,8},{8,4},{12,0},{16,28},{20,24},{24,20},{28,16},{1,13},{... | collective-permute-start | bytes 983048 | tf_op jit(solution)/shard_map/ppermute | solution.py:20
  6.3 14.9 %collective-permute-start.1 = (bf16[128,1280]{1,0:T(8,128)(2,1)S(1)}, bf16[128,1280]{1,0:T(8,128)(2,1)S(1)}, u32[]{:S(2)}, u32[]{:S(2)}) collective-permute-start(bf16[128,1280]{1,0:T(8,128)(2,1)S(1)} %pad_maximum_fusion.7), channel_id=1, source_target_pairs={{0,8},{4,12},{8,0},{12,4},{16,24},{20,28},{24,16},{28,20},{1,9},{5... | collective-permute-start | bytes 983048 | tf_op jit(solution)/shard_map/ppermute | solution.py:20
  6.8 15.1 %collective-permute-start = (bf16[128,1280]{1,0:T(8,128)(2,1)S(1)}, bf16[128,1280]{1,0:T(8,128)(2,1)S(1)}, u32[]{:S(2)}, u32[]{:S(2)}) collective-permute-start(bf16[128,1280]{1,0:T(8,128)(2,1)S(1)} %pad_maximum_fusion.6), channel_id=1, source_target_pairs={{0,4},{4,0},{8,12},{12,8},{16,20},{20,16},{24,28},{28,24},{1,5},{5... | collective-permute-start | bytes 983048 | tf_op jit(solution)/shard_map/ppermute | solution.py:20
  24.9 12.2 %collective-permute-start.3 = (bf16[3,128,640]{2,1,0:T(8,128)(2,1)S(1)}, bf16[3,128,640]{2,1,0:T(8,128)(2,1)S(1)}, u32[]{:S(2)}, u32[]{:S(2)}) collective-permute-start(bf16[3,128,640]{2,1,0:T(8,128)(2,1)S(1)} %get-tuple-element.75), channel_id=1, source_target_pairs={{0,2},{1,3},{2,0},{3,1},{4,6},{5,7},{6,4},{7,5},{8,10},{9,11},{10,... | collective-permute-start | bytes 1474568 | tf_op jit(solution)/shard_map/ppermute | solution.py:20
  27.6 73.6 %collective-permute-start.8 = (bf16[512,768]{1,0:T(8,128)(2,1)}, bf16[512,768]{1,0:T(8,128)(2,1)}, u32[]{:S(2)}, u32[]{:S(2)}) collective-permute-start(bf16[512,768]{1,0:T(8,128)(2,1)} %get-tuple-element.64), channel_id=1, source_target_pairs={{0,4},{4,0},{8,12},{12,8},{16,20},{20,16},{24,28},{28,24},{1,5},{5... | collective-permute-start | bytes 2359304 | tf_op jit(solution)/shard_map/ppermute | solution.py:20
  28.4 59.0 %collective-permute-start.9 = (bf16[512,768]{1,0:T(8,128)(2,1)}, bf16[512,768]{1,0:T(8,128)(2,1)}, u32[]{:S(2)}, u32[]{:S(2)}) collective-permute-start(bf16[512,768]{1,0:T(8,128)(2,1)} %get-tuple-element.64), channel_id=1, source_target_pairs={{0,8},{4,12},{8,0},{12,4},{16,24},{20,28},{24,16},{28,20},{1,9},{5... | collective-permute-start | bytes 2359304 | tf_op jit(solution)/shard_map/ppermute | solution.py:20
  29.9 30.9 %collective-permute-start.14 = (bf16[192,1536]{1,0:T(8,128)(2,1)}, bf16[192,1536]{1,0:T(8,128)(2,1)}, u32[]{:S(2)}, u32[]{:S(2)}) collective-permute-start(bf16[192,1536]{1,0:T(8,128)(2,1)} %param.11), channel_id=1, source_target_pairs={{0,16},{4,20},{8,24},{12,28},{16,0},{20,4},{24,8},{28,12},{1,17},{... | collective-permute-start | bytes 1769480 | tf_op jit(solution)/shard_map/ppermute | solution.py:20
  32.5 44.5 %collective-permute-start.6 = (bf16[512,768]{1,0:T(8,128)(2,1)}, bf16[512,768]{1,0:T(8,128)(2,1)}, u32[]{:S(2)}, u32[]{:S(2)}) collective-permute-start(bf16[512,768]{1,0:T(8,128)(2,1)} %get-tuple-element.65), channel_id=1, source_target_pairs={{0,8},{4,12},{8,0},{12,4},{16,24},{20,28},{24,16},{28,20},{1,9},{5... | collective-permute-start | bytes 2359304 | tf_op jit(solution)/shard_map/ppermute | solution.py:20
  38.2 39.4 %collective-permute-start.4 = (bf16[2,3,128,640]{3,2,1,0:T(8,128)(2,1)}, bf16[2,3,128,640]{3,2,1,0:T(8,128)(2,1)}, u32[]{:S(2)}, u32[]{:S(2)}) collective-permute-start(bf16[2,3,128,640]{3,2,1,0:T(8,128)(2,1)} %pad_maximum_fusion), channel_id=1, source_target_pairs={{0,1},{1,0},{2,3},{3,2},{4,5},{5,4},{6,7},{7,6},{8,9},{9,8},{10,11... | collective-permute-start | bytes 2949128 | tf_op jit(solution)/shard_map/ppermute | solution.py:20
  60.8 21.0 %collective-permute-start.5 = (bf16[512,768]{1,0:T(8,128)(2,1)}, bf16[512,768]{1,0:T(8,128)(2,1)S(1)}, u32[]{:S(2)}, u32[]{:S(2)}) collective-permute-start(bf16[512,768]{1,0:T(8,128)(2,1)} %get-tuple-element.65), channel_id=1, source_target_pairs={{0,4},{4,0},{8,12},{12,8},{16,20},{20,16},{24,28},{28,24},{1,5},{5... | collective-permute-start | bytes 2359304 | tf_op jit(solution)/shard_map/ppermute | solution.py:20
  77.1 67.0 %collective-permute-start.11 = (bf16[3,128,640]{2,1,0:T(8,128)(2,1)S(1)}, bf16[3,128,640]{2,1,0:T(8,128)(2,1)S(1)}, u32[]{:S(2)}, u32[]{:S(2)}) collective-permute-start(bf16[3,128,640]{2,1,0:T(8,128)(2,1)S(1)} %get-tuple-element.72), channel_id=1, source_target_pairs={{0,2},{1,3},{2,0},{3,1},{4,6},{5,7},{6,4},{7,5},{8,10},{9,11},{10,... | collective-permute-start | bytes 1474568 | tf_op jit(solution)/shard_map/ppermute | solution.py:20
  77.6 20.6 %collective-permute-start.7 = (bf16[512,768]{1,0:T(8,128)(2,1)}, bf16[512,768]{1,0:T(8,128)(2,1)S(1)}, u32[]{:S(2)}, u32[]{:S(2)}) collective-permute-start(bf16[512,768]{1,0:T(8,128)(2,1)} %collective-permute-done.6), channel_id=1, source_target_pairs={{0,4},{4,0},{8,12},{12,8},{16,20},{20,16},{24,28},{28,24},{1,5},{5... | collective-permute-start | bytes 2359304 | tf_op jit(solution)/shard_map/ppermute | solution.py:20
  81.9 64.2 %collective-permute-start.16 = (bf16[384,1536]{1,0:T(8,128)(2,1)S(1)}, bf16[384,1536]{1,0:T(8,128)(2,1)S(1)}, u32[]{:S(2)}, u32[]{:S(2)}) collective-permute-start(bf16[384,1536]{1,0:T(8,128)(2,1)S(1)} %get-tuple-element.66), channel_id=1, source_target_pairs={{0,4},{4,0},{8,12},{12,8},{16,20},{20,16},{24,28},{28,24},{1,5},{5... | collective-permute-start | bytes 3538952 | tf_op jit(solution)/shard_map/ppermute | solution.py:20
  87.4 56.9 %collective-permute-start.15 = (bf16[384,1536]{1,0:T(8,128)(2,1)S(1)}, bf16[384,1536]{1,0:T(8,128)(2,1)}, u32[]{:S(2)}, u32[]{:S(2)}) collective-permute-start(bf16[384,1536]{1,0:T(8,128)(2,1)S(1)} %get-tuple-element.66), channel_id=1, source_target_pairs={{0,8},{4,12},{8,0},{12,4},{16,24},{20,28},{24,16},{28,20},{1,9},{5... | collective-permute-start | bytes 3538952 | tf_op jit(solution)/shard_map/ppermute | solution.py:20
  98.2 39.5 %collective-permute-start.10 = (bf16[512,768]{1,0:T(8,128)(2,1)}, bf16[512,768]{1,0:T(8,128)(2,1)S(1)}, u32[]{:S(2)}, u32[]{:S(2)}) collective-permute-start(bf16[512,768]{1,0:T(8,128)(2,1)} %collective-permute-done.9), channel_id=1, source_target_pairs={{0,4},{4,0},{8,12},{12,8},{16,20},{20,16},{24,28},{28,24},{1,5},{5... | collective-permute-start | bytes 2359304 | tf_op jit(solution)/shard_map/ppermute | solution.py:20
  101.2 47.6 %collective-permute-start.18 = (bf16[640,768]{1,0:T(8,128)(2,1)S(1)}, bf16[640,768]{1,0:T(8,128)(2,1)S(1)}, u32[]{:S(2)}, u32[]{:S(2)}) collective-permute-start(bf16[640,768]{1,0:T(8,128)(2,1)S(1)} %add_convert_fusion.1), channel_id=1, source_target_pairs={{0,16},{4,20},{8,24},{12,28},{16,0},{20,4},{24,8},{28,12},{1,17},{... | collective-permute-start | bytes 2949128 | tf_op jit(solution)/shard_map/ppermute | solution.py:20
  141.5 58.6 %collective-permute-start.13 = (bf16[256,768]{1,0:T(8,128)(2,1)}, bf16[256,768]{1,0:T(8,128)(2,1)}, u32[]{:S(2)}, u32[]{:S(2)}) collective-permute-start(bf16[256,768]{1,0:T(8,128)(2,1)} %slice.376), channel_id=1, source_target_pairs={{0,16},{4,20},{8,24},{12,28},{16,0},{20,4},{24,8},{28,12},{1,17},{... | collective-permute-start | bytes 1179656 | tf_op jit(solution)/shard_map/ppermute | solution.py:20
  144.3 51.5 %collective-permute-start.19 = (bf16[384,1536]{1,0:T(8,128)(2,1)}, bf16[384,1536]{1,0:T(8,128)(2,1)}, u32[]{:S(2)}, u32[]{:S(2)}) collective-permute-start(bf16[384,1536]{1,0:T(8,128)(2,1)} %collective-permute-done.15), channel_id=1, source_target_pairs={{0,4},{4,0},{8,12},{12,8},{16,20},{20,16},{24,28},{28,24},{1,5},{5... | collective-permute-start | bytes 3538952 | tf_op jit(solution)/shard_map/ppermute | solution.py:20
  146.1 38.8 %collective-permute-start.17 = (bf16[384,768]{1,0:T(8,128)(2,1)}, bf16[384,768]{1,0:T(8,128)(2,1)}, u32[]{:S(2)}, u32[]{:S(2)}) collective-permute-start(bf16[384,768]{1,0:T(8,128)(2,1)} %slice.386), channel_id=1, source_target_pairs={{0,16},{4,20},{8,24},{12,28},{16,0},{20,4},{24,8},{28,12},{1,17},{... | collective-permute-start | bytes 1769480 | tf_op jit(solution)/shard_map/ppermute | solution.py:20
  209.4 5.9 %collective-permute-start.20 = (bf16[8,2,48,384]{3,2,1,0:T(8,128)(2,1)}, bf16[8,2,48,384]{3,2,1,0:T(8,128)(2,1)S(1)}, u32[]{:S(2)}, u32[]{:S(2)}) collective-permute-start(bf16[8,2,48,384]{3,2,1,0:T(8,128)(2,1)} %pad_maximum_fusion.2), channel_id=1, source_target_pairs={{0,1},{1,0},{2,3},{3,2},{4,5},{5,4},{6,7},{7,6},{8,9},{9,8},{10,11... | collective-permute-start | bytes 1769480 | tf_op jit(solution)/shard_map/ppermute | solution.py:20
  213.7 7.0 %collective-permute-start.26 = (bf16[8,1,48,256]{3,2,1,0:T(8,128)(2,1)S(1)}, bf16[8,1,48,256]{3,2,1,0:T(8,128)(2,1)S(1)}, u32[]{:S(2)}, u32[]{:S(2)}) collective-permute-start(bf16[8,1,48,256]{3,2,1,0:T(8,128)(2,1)S(1)} %pad_maximum_fusion.10), channel_id=1, source_target_pairs={{0,2},{1,3},{2,0},{3,1},{4,6},{5,7},{6,4},{7,5},{8,10},{9,11},{10,... | collective-permute-start | bytes 589832 | tf_op jit(solution)/shard_map/ppermute | solution.py:20
  220.9 7.0 %collective-permute-start.27 = (bf16[4,48,256]{2,1,0:T(8,128)(2,1)S(1)}, bf16[4,48,256]{2,1,0:T(8,128)(2,1)S(1)}, u32[]{:S(2)}, u32[]{:S(2)}) collective-permute-start(bf16[4,48,256]{2,1,0:T(8,128)(2,1)S(1)} %pad_maximum_fusion.14), channel_id=1, source_target_pairs={{0,16},{4,20},{8,24},{12,28},{16,0},{20,4},{24,8},{28,12},{1,17},{... | collective-permute-start | bytes 294920 | tf_op jit(solution)/shard_map/ppermute | solution.py:20
  221.0 14.0 %collective-permute-start.21 = (bf16[8,1,48,384]{3,2,1,0:T(8,128)(2,1)S(1)}, bf16[8,1,48,384]{3,2,1,0:T(8,128)(2,1)S(1)}, u32[]{:S(2)}, u32[]{:S(2)}) collective-permute-start(bf16[8,1,48,384]{3,2,1,0:T(8,128)(2,1)S(1)} %pad_maximum_fusion.9), channel_id=1, source_target_pairs={{0,2},{1,3},{2,0},{3,1},{4,6},{5,7},{6,4},{7,5},{8,10},{9,11},{10,... | collective-permute-start | bytes 884744 | tf_op jit(solution)/shard_map/ppermute | solution.py:20
  235.2 7.8 %collective-permute-start.22 = (bf16[4,48,384]{2,1,0:T(8,128)(2,1)S(1)}, bf16[4,48,384]{2,1,0:T(8,128)(2,1)S(1)}, u32[]{:S(2)}, u32[]{:S(2)}) collective-permute-start(bf16[4,48,384]{2,1,0:T(8,128)(2,1)S(1)} %pad_maximum_fusion.11), channel_id=1, source_target_pairs={{0,16},{4,20},{8,24},{12,28},{16,0},{20,4},{24,8},{28,12},{1,17},{... | collective-permute-start | bytes 442376 | tf_op jit(solution)/shard_map/ppermute | solution.py:20
  (26 other events, 140.2 us)

commit v2 on v1

--- a/solution.py
+++ b/solution.py
@@ -56,7 +56,8 @@
 def adam(own, recvs, state, previous, row, column):
     rows, width = recvs[0].shape if recvs else own.shape
     full = state[0].shape
-    tile = math.gcd(math.gcd(rows, row), TILE) if rows % TILE == 0 else rows
+    common = math.gcd(rows, row)
+    tile = max(d for d in range(1, TILE + 1) if common % d == 0)
     here = pl.BlockSpec((tile, width), lambda i: (i, 0))
     below = pl.BlockSpec((tile, width), lambda i: (i + row // tile, 0))
     there = pl.BlockSpec((tile, width), lambda i: (i + row // tile, column // width))
@@ -174,18 +175,17 @@
         own = lax.dynamic_slice(cotangent, (0, ((k ^ c) * GROUP + m) * rows), (tokens, rows))
         if after is not None:
             own = gate(own, after)
-        acc = dot_tokens(own, blocks[j])
-        firsts[j] = acc
-        acc = acc + dot_tokens(cots[0], ahead[j]) + dot_tokens(cots[1], side[j])
+        partial[j] = dot_tokens(own, blocks[j])
+        acc = partial[j] + dot_tokens(cots[0], ahead[j]) + dot_tokens(cots[1], side[j])
         return acc + dot_tokens(cots[2], gate(diagonal[j], acc))
 
-    firsts = {}
+    partial = {}
     last = COLUMN_PARTS - 1
     parts = row_parts(rows)
     cots_away = cotangents("a", across_of["a"])
     sent = [group_sum(0, c, cots_away[i], None).astype(jnp.bfloat16) for i, c in enumerate(away)]
     received = {(0, 0): [swap(x, "dp", c * GROUP) for x, c in zip(sent, away)]}
-    mark, early_mark = sent[-1], firsts[0]
+    mark = sent[-1]
 
     cots_home = cotangents("h", gate(across_of["h"], mark))
     own_sums = [group_sum(0, 0, cots_home[0], mark)]
@@ -194,7 +194,7 @@
         for start, size in parts if j == last else [(0, rows)]:
             sent = [x[start : start + size].astype(jnp.bfloat16) for x in sums]
             received[j, start] = [swap(x, "dp", c * GROUP) for x, c in zip(sent, away)]
-        mark = sent[-1]
+        mark, early_mark = sent[-1], partial[1]
         own_sums.append(group_sum(j, 0, cots_home[0], mark))
 
     seen, held, bit = [0], [prompts], n // 2
@@ -208,12 +208,13 @@
     far = held[-1]
 
     near_other = swap(near, "dp", 1)
+    mark = own_sums[-1]
     new_state, weights = None, []
     for j in range(last):
         recvs = [gate(x, mark) for x in received[j, 0]]
         *new_state, weight = adam(own_sums[j], recvs, state, new_state, 0, j * part_width)
         weights.append(weight)
-    far = gate(far, mark)
+    far = gate(far, weights[-1])
     far_other = swap(far, "dp", 1)
     seen += [q ^ 1 for q in seen]
 

time: 257 us -> 291 us (1.13)
  waiting for transfers between devices: 128 us -> 171 us
  matrix products: 44.2 us -> 36.7 us
  starting transfers between devices: 34.6 us -> 31.1 us
    ppermute x30, waiting for transfers between devices: 128 us -> 171 us  [swap(): return lax.ppermute(x, axis, [(i, i ^ bit) for i in range(n)])]
    dot_general x16, matrix products: 27.9 us -> 22.4 us  [dot_tokens(): lax.dot_general(cot, acts, (((0,), (0,)), ((), ())), preferred_element_ty...]
    unnamed x56 -> x60, local copies, waits for them, and re-layouts: 4.95 us -> 8.66 us
    ppermute x30, starting transfers between devices: 34.6 us -> 31.1 us  [swap(): return lax.ppermute(x, axis, [(i, i ^ bit) for i in range(n)])]
  transfers between devices with their start and end apart: 30 -> 30, of which waited for: 15 -> 18; matrix products, arithmetic and copies ran while one was open for 24% -> 18% of each run, Pallas kernels for 5% -> 5%
where the time goes in v2:
time: 291 us; the launch traced here: 290 us
  waiting for transfers between devices  171 us (59%)
  matrix products  36.7 us (13%)
  starting transfers between devices  31.1 us (11%)
  local copies, waits for them, and re-layouts  24.1 us (8%)
  Pallas kernels  18.9 us (6%)
  other arithmetic  5.97 us (2%)
    ppermute x30, waiting for transfers between devices, swap(): return lax.ppermute(x, axis, [(i, i ^ bit) for i in range(n)])  171 us
    ppermute x30, starting transfers between devices, swap(): return lax.ppermute(x, axis, [(i, i ^ bit) for i in range(n)])  31.1 us
    dot_general x16, matrix products, dot_tokens(): lax.dot_general(cot, acts, (((0,), (0,)), ((), ())), preferred_element_ty...  22.4 us
    pallas_call x3, Pallas kernels, adam(): pl.pallas_call(functools.partial(adam_kernel, len(recvs)), grid=(rows //...  17.1 us
    dot_general x6, matrix products, dot_features(): lax.dot_general(rows, weight, (((1,), (1,)), ((), ())), preferred_element...  14.3 us
    unnamed x60, local copies, waits for them, and re-layouts  8.66 us
  transfers between devices with their start and end apart: 30, of which 18 were waited for; matrix products, arithmetic and copies ran while one was open for 18% of the time, Pallas kernels for 5%

profile of v2, /device:TPU:0, one launch (start us, length us, event | category | flops | bytes accessed | tf_op | source)
XLA Modules:
  0.0 289.6 jit_solution(5381162545194690773)
XLA Ops:
  2.2 4.1 %collective-permute-start.2 = (bf16[128,1280]{1,0:T(8,128)(2,1)S(1)}, bf16[128,1280]{1,0:T(8,128)(2,1)S(1)}, u32[]{:S(2)}, u32[]{:S(2)}) collective-permute-start(bf16[128,1280]{1,0:T(8,128)(2,1)S(1)} %pad_maximum_fusion.8), channel_id=1, source_target_pairs={{0,12},{4,8},{8,4},{12,0},{16,28},{20,24},{24,20},{28,16},{1,13},{... | collective-permute-start | bytes 983048 | tf_op jit(solution)/shard_map/ppermute | solution.py:20
  7.0 7.8 %collective-permute-done.2 = bf16[128,1280]{1,0:T(8,128)(2,1)S(1)} collective-permute-done((bf16[128,1280]{1,0:T(8,128)(2,1)S(1)}, bf16[128,1280]{1,0:T(8,128)(2,1)S(1)}, u32[]{:S(2)}, u32[]{:S(2)}) %collective-permute-start.2) | collective-permute-done | bytes 327712 | tf_op jit(solution)/shard_map/ppermute | solution.py:20
  15.5 5.6 %collective-permute-done.1 = bf16[128,1280]{1,0:T(8,128)(2,1)S(1)} collective-permute-done((bf16[128,1280]{1,0:T(8,128)(2,1)S(1)}, bf16[128,1280]{1,0:T(8,128)(2,1)S(1)}, u32[]{:S(2)}, u32[]{:S(2)}) %collective-permute-start.1) | collective-permute-done | bytes 327712 | tf_op jit(solution)/shard_map/ppermute | solution.py:20
  24.5 10.7 %collective-permute-done.3 = bf16[3,128,640]{2,1,0:T(8,128)(2,1)S(1)} collective-permute-done((bf16[3,128,640]{2,1,0:T(8,128)(2,1)S(1)}, bf16[3,128,640]{2,1,0:T(8,128)(2,1)S(1)}, u32[]{:S(2)}, u32[]{:S(2)}) %collective-permute-start.3) | collective-permute-done | bytes 491552 | tf_op jit(solution)/shard_map/ppermute | solution.py:20
  41.5 2.6 collective-permute-start.14
  53.2 20.2 %collective-permute-done.6 = bf16[512,768]{1,0:T(8,128)(2,1)} collective-permute-done((bf16[512,768]{1,0:T(8,128)(2,1)}, bf16[512,768]{1,0:T(8,128)(2,1)}, u32[]{:S(2)}, u32[]{:S(2)}) %collective-permute-start.6) | collective-permute-done | bytes 786464 | tf_op jit(solution)/shard_map/ppermute | solution.py:20
  77.7 11.7 %collective-permute-done.9 = bf16[512,768]{1,0:T(8,128)(2,1)} collective-permute-done((bf16[512,768]{1,0:T(8,128)(2,1)}, bf16[512,768]{1,0:T(8,128)(2,1)}, u32[]{:S(2)}, u32[]{:S(2)}) %collective-permute-start.9) | collective-permute-done | bytes 786464 | tf_op jit(solution)/shard_map/ppermute | solution.py:20
  95.1 15.7 %collective-permute-done.7 = bf16[512,768]{1,0:T(8,128)(2,1)S(1)} collective-permute-done((bf16[512,768]{1,0:T(8,128)(2,1)}, bf16[512,768]{1,0:T(8,128)(2,1)S(1)}, u32[]{:S(2)}, u32[]{:S(2)}) %collective-permute-start.7) | collective-permute-done | bytes 786464 | tf_op jit(solution)/shard_map/ppermute | solution.py:20
  116.6 8.7 %collective-permute-done.10 = bf16[512,768]{1,0:T(8,128)(2,1)S(1)} collective-permute-done((bf16[512,768]{1,0:T(8,128)(2,1)}, bf16[512,768]{1,0:T(8,128)(2,1)S(1)}, u32[]{:S(2)}, u32[]{:S(2)}) %collective-permute-start.10) | collective-permute-done | bytes 786464 | tf_op jit(solution)/shard_map/ppermute | solution.py:20
  145.0 17.2 %collective-permute-done.16.refs_1_ = bf16[640,768]{1,0:T(8,128)(2,1)S(1)} collective-permute-done((bf16[640,768]{1,0:T(8,128)(2,1)S(1)}, bf16[640,768]{1,0:T(8,128)(2,1)S(1)}, u32[]{:S(2)}, u32[]{:S(2)}) %collective-permute-start.16) | collective-permute-done | bytes 983072 | tf_op jit(solution)/shard_map/ppermute | solution.py:20
  165.3 8.5 %adam.3 = (f32[640,1536]{1,0:T(8,128)}, f32[640,1536]{1,0:T(8,128)}, f32[640,1536]{1,0:T(8,128)}, bf16[640,768]{1,0:T(8,128)(2,1)}) custom-call(f32[640,768]{1,0:T(8,128)} %convolution_add_fusion.2.refs_0_, bf16[640,768]{1,0:T(8,128)(2,1)} %copy-done.14, f32[640,1536]{1,0:T(8,128)} %refs_2_.5, f32[640,1536]{1,0:T(8,128)} %refs_3_.5, f32[640,1536]{1,0:T(8,128)} %refs_4_.5), custom_call_target="tpu_custom_call" | custom-call | flops 9830400 | bytes 15728640 | tf_op jit(solution)/shard_map/adam/pallas_call | solution.py:66
  173.7 28.8 %collective-permute-done.15 = bf16[384,1536]{1,0:T(8,128)(2,1)} collective-permute-done((bf16[384,1536]{1,0:T(8,128)(2,1)}, bf16[384,1536]{1,0:T(8,128)(2,1)}, u32[]{:S(2)}, u32[]{:S(2)}) %collective-permute-start.15) | collective-permute-done | bytes 1179680 | tf_op jit(solution)/shard_map/ppermute | solution.py:20
  206.8 3.2 %fusion = f32[1152,640]{1,0:T(8,128)} fusion(bf16[640,768]{1,0:T(8,128)(2,1)S(1)} %copy-done.15, bf16[1152,1536]{1,0:T(8,128)(2,1)S(1)} %constant_dynamic-update-slice_fusion.2), kind=kOutput, calls=%fused_computation.8 | convolution fusion | flops 1132462080 | bytes 5701632 | tf_op jit(solution)/shard_map/dot_general | solution.py:28
  210.0 5.3 %adam.4 = (f32[640,1536]{1,0:T(8,128)}, f32[640,1536]{1,0:T(8,128)}, f32[640,1536]{1,0:T(8,128)}, bf16[384,768]{1,0:T(8,128)(2,1)}) custom-call(f32[640,768]{1,0:T(8,128)} %convolution_add_fusion.3.refs_0_, bf16[384,768]{1,0:T(8,128)(2,1)} %collective-permute-done.18.refs_1_, ...), custom_call_target="tpu_custom_call", output_to_operand_aliasing={{0}: (5, {}), {1}: (6, {}), {2}: (7, {})} | custom-call | flops 5898240 | bytes 9437184 | tf_op jit(solution)/shard_map/adam/pallas_call | solution.py:66
  215.4 3.4 %convolution_add_fusion = f32[1152,384]{1,0:T(8,128)S(1)} fusion(bf16[384,768]{1,0:T(8,128)(2,1)} %get-tuple-element.46, f32[1152,640]{1,0:T(8,128)} %fusion, bf16[1152,1536]{1,0:T(8,128)(2,1)} %copy-done.6), kind=kOutput, calls=%fused_computation | convolution fusion | flops 679919616 | bytes 5898240 | tf_op jit(solution)/shard_map/dot_general | solution.py:28
  218.8 11.5 %collective-permute-done.19 = bf16[384,1536]{1,0:T(8,128)(2,1)} collective-permute-done((bf16[384,1536]{1,0:T(8,128)(2,1)}, bf16[384,1536]{1,0:T(8,128)(2,1)}, u32[]{:S(2)}, u32[]{:S(2)}) %collective-permute-start.19) | collective-permute-done | bytes 1179680 | tf_op jit(solution)/shard_map/ppermute | solution.py:20
  234.6 3.3 %adam.5 = (f32[640,1536]{1,0:T(8,128)}, f32[640,1536]{1,0:T(8,128)}, f32[640,1536]{1,0:T(8,128)}, bf16[256,768]{1,0:T(8,128)(2,1)}) custom-call(f32[640,768]{1,0:T(8,128)} %convolution_add_fusion.3.refs_0_, bf16[256,768]{1,0:T(8,128)(2,1)} %collective-permute-done.13.refs_1_, ...), custom_call_target="tpu_custom_call", output_to_operand_aliasing={{0}: (5, {}), {1}: (6, {}), {2}: (7, {})} | custom-call | flops 3932160 | bytes 6291456 | tf_op jit(solution)/shard_map/adam/pallas_call | solution.py:66
  237.9 2.6 convolution_add_fusion.1
  250.1 5.1 %collective-permute-done.26 = bf16[8,1,48,256]{3,2,1,0:T(8,128)(2,1)S(1)} collective-permute-done((bf16[8,1,48,256]{3,2,1,0:T(8,128)(2,1)S(1)}, bf16[8,1,48,256]{3,2,1,0:T(8,128)(2,1)S(1)}, u32[]{:S(2)}, u32[]{:S(2)}) %collective-permute-start.26) | collective-permute-done | bytes 196640 | tf_op jit(solution)/shard_map/ppermute | solution.py:20
  257.0 4.6 %collective-permute-done.27 = bf16[4,48,256]{2,1,0:T(8,128)(2,1)S(1)} collective-permute-done((bf16[4,48,256]{2,1,0:T(8,128)(2,1)S(1)}, bf16[4,48,256]{2,1,0:T(8,128)(2,1)S(1)}, u32[]{:S(2)}, u32[]{:S(2)}) %collective-permute-start.27) | collective-permute-done | bytes 98336 | tf_op jit(solution)/shard_map/ppermute | solution.py:20
  261.7 4.6 %collective-permute-done.28 = bf16[4,48,256]{2,1,0:T(8,128)(2,1)S(1)} collective-permute-done((bf16[4,48,256]{2,1,0:T(8,128)(2,1)S(1)}, bf16[4,48,256]{2,1,0:T(8,128)(2,1)S(1)}, u32[]{:S(2)}, u32[]{:S(2)}) %collective-permute-start.28) | collective-permute-done | bytes 98336 | tf_op jit(solution)/shard_map/ppermute | solution.py:20
  271.1 5.3 %collective-permute-done.22 = bf16[4,48,384]{2,1,0:T(8,128)(2,1)S(1)} collective-permute-done((bf16[4,48,384]{2,1,0:T(8,128)(2,1)S(1)}, bf16[4,48,384]{2,1,0:T(8,128)(2,1)S(1)}, u32[]{:S(2)}, u32[]{:S(2)}) %collective-permute-start.22) | collective-permute-done | bytes 147488 | tf_op jit(solution)/shard_map/ppermute | solution.py:20
  276.5 5.2 %collective-permute-done.23 = bf16[4,48,384]{2,1,0:T(8,128)(2,1)S(1)} collective-permute-done((bf16[4,48,384]{2,1,0:T(8,128)(2,1)S(1)}, bf16[4,48,384]{2,1,0:T(8,128)(2,1)S(1)}, u32[]{:S(2)}, u32[]{:S(2)}) %collective-permute-start.23) | collective-permute-done | bytes 147488 | tf_op jit(solution)/shard_map/ppermute | solution.py:20
  282.2 4.8 %collective-permute-done.24 = bf16[4,48,384]{2,1,0:T(8,128)(2,1)S(1)} collective-permute-done((bf16[4,48,384]{2,1,0:T(8,128)(2,1)S(1)}, bf16[4,48,384]{2,1,0:T(8,128)(2,1)S(1)}, u32[]{:S(2)}, u32[]{:S(2)}) %collective-permute-start.24) | collective-permute-done | bytes 147488 | tf_op jit(solution)/shard_map/ppermute | solution.py:20
  (187 shorter events, 87.6 us)
Async XLA Ops:
  2.2 12.7 %collective-permute-start.2 = (bf16[128,1280]{1,0:T(8,128)(2,1)S(1)}, bf16[128,1280]{1,0:T(8,128)(2,1)S(1)}, u32[]{:S(2)}, u32[]{:S(2)}) collective-permute-start(bf16[128,1280]{1,0:T(8,128)(2,1)S(1)} %pad_maximum_fusion.8), channel_id=1, source_target_pairs={{0,12},{4,8},{8,4},{12,0},{16,28},{20,24},{24,20},{28,16},{1,13},{... | collective-permute-start | bytes 983048 | tf_op jit(solution)/shard_map/ppermute | solution.py:20
  6.3 14.9 %collective-permute-start.1 = (bf16[128,1280]{1,0:T(8,128)(2,1)S(1)}, bf16[128,1280]{1,0:T(8,128)(2,1)S(1)}, u32[]{:S(2)}, u32[]{:S(2)}) collective-permute-start(bf16[128,1280]{1,0:T(8,128)(2,1)S(1)} %pad_maximum_fusion.7), channel_id=1, source_target_pairs={{0,8},{4,12},{8,0},{12,4},{16,24},{20,28},{24,16},{28,20},{1,9},{5... | collective-permute-start | bytes 983048 | tf_op jit(solution)/shard_map/ppermute | solution.py:20
  6.8 15.1 %collective-permute-start = (bf16[128,1280]{1,0:T(8,128)(2,1)S(1)}, bf16[128,1280]{1,0:T(8,128)(2,1)S(1)}, u32[]{:S(2)}, u32[]{:S(2)}) collective-permute-start(bf16[128,1280]{1,0:T(8,128)(2,1)S(1)} %pad_maximum_fusion.6), channel_id=1, source_target_pairs={{0,4},{4,0},{8,12},{12,8},{16,20},{20,16},{24,28},{28,24},{1,5},{5... | collective-permute-start | bytes 983048 | tf_op jit(solution)/shard_map/ppermute | solution.py:20
  22.9 12.3 %collective-permute-start.3 = (bf16[3,128,640]{2,1,0:T(8,128)(2,1)S(1)}, bf16[3,128,640]{2,1,0:T(8,128)(2,1)S(1)}, u32[]{:S(2)}, u32[]{:S(2)}) collective-permute-start(bf16[3,128,640]{2,1,0:T(8,128)(2,1)S(1)} %get-tuple-element.75), channel_id=1, source_target_pairs={{0,2},{1,3},{2,0},{3,1},{4,6},{5,7},{6,4},{7,5},{8,10},{9,11},{10,... | collective-permute-start | bytes 1474568 | tf_op jit(solution)/shard_map/ppermute | solution.py:20
  37.1 36.7 %collective-permute-start.4 = (bf16[2,3,128,640]{3,2,1,0:T(8,128)(2,1)}, bf16[2,3,128,640]{3,2,1,0:T(8,128)(2,1)}, u32[]{:S(2)}, u32[]{:S(2)}) collective-permute-start(bf16[2,3,128,640]{3,2,1,0:T(8,128)(2,1)} %pad_maximum_fusion), channel_id=1, source_target_pairs={{0,1},{1,0},{2,3},{3,2},{4,5},{5,4},{6,7},{7,6},{8,9},{9,8},{10,11... | collective-permute-start | bytes 2949128 | tf_op jit(solution)/shard_map/ppermute | solution.py:20
  38.3 52.6 %collective-permute-start.5 = (bf16[512,768]{1,0:T(8,128)(2,1)}, bf16[512,768]{1,0:T(8,128)(2,1)}, u32[]{:S(2)}, u32[]{:S(2)}) collective-permute-start(bf16[512,768]{1,0:T(8,128)(2,1)} %get-tuple-element.65), channel_id=1, source_target_pairs={{0,4},{4,0},{8,12},{12,8},{16,20},{20,16},{24,28},{28,24},{1,5},{5... | collective-permute-start | bytes 2359304 | tf_op jit(solution)/shard_map/ppermute | solution.py:20
  39.9 33.4 %collective-permute-start.6 = (bf16[512,768]{1,0:T(8,128)(2,1)}, bf16[512,768]{1,0:T(8,128)(2,1)}, u32[]{:S(2)}, u32[]{:S(2)}) collective-permute-start(bf16[512,768]{1,0:T(8,128)(2,1)} %get-tuple-element.65), channel_id=1, source_target_pairs={{0,8},{4,12},{8,0},{12,4},{16,24},{20,28},{24,16},{28,20},{1,9},{5... | collective-permute-start | bytes 2359304 | tf_op jit(solution)/shard_map/ppermute | solution.py:20
  41.5 87.9 %collective-permute-start.14 = (bf16[192,1536]{1,0:T(8,128)(2,1)}, bf16[192,1536]{1,0:T(8,128)(2,1)}, u32[]{:S(2)}, u32[]{:S(2)}) collective-permute-start(bf16[192,1536]{1,0:T(8,128)(2,1)} %param.11), channel_id=1, source_target_pairs={{0,16},{4,20},{8,24},{12,28},{16,0},{20,4},{24,8},{28,12},{1,17},{... | collective-permute-start | bytes 1769480 | tf_op jit(solution)/shard_map/ppermute | solution.py:20
  44.1 45.3 %collective-permute-start.9 = (bf16[512,768]{1,0:T(8,128)(2,1)}, bf16[512,768]{1,0:T(8,128)(2,1)}, u32[]{:S(2)}, u32[]{:S(2)}) collective-permute-start(bf16[512,768]{1,0:T(8,128)(2,1)} %get-tuple-element.64), channel_id=1, source_target_pairs={{0,8},{4,12},{8,0},{12,4},{16,24},{20,28},{24,16},{28,20},{1,9},{5... | collective-permute-start | bytes 2359304 | tf_op jit(solution)/shard_map/ppermute | solution.py:20
  73.3 40.7 %collective-permute-start.8 = (bf16[512,768]{1,0:T(8,128)(2,1)}, bf16[512,768]{1,0:T(8,128)(2,1)S(1)}, u32[]{:S(2)}, u32[]{:S(2)}) collective-permute-start(bf16[512,768]{1,0:T(8,128)(2,1)} %get-tuple-element.64), channel_id=1, source_target_pairs={{0,4},{4,0},{8,12},{12,8},{16,20},{20,16},{24,28},{28,24},{1,5},{5... | collective-permute-start | bytes 2359304 | tf_op jit(solution)/shard_map/ppermute | solution.py:20
  73.7 37.1 %collective-permute-start.7 = (bf16[512,768]{1,0:T(8,128)(2,1)}, bf16[512,768]{1,0:T(8,128)(2,1)S(1)}, u32[]{:S(2)}, u32[]{:S(2)}) collective-permute-start(bf16[512,768]{1,0:T(8,128)(2,1)} %collective-permute-done.6), channel_id=1, source_target_pairs={{0,4},{4,0},{8,12},{12,8},{16,20},{20,16},{24,28},{28,24},{1,5},{5... | collective-permute-start | bytes 2359304 | tf_op jit(solution)/shard_map/ppermute | solution.py:20
  89.4 40.0 %collective-permute-start.11 = (bf16[3,128,640]{2,1,0:T(8,128)(2,1)S(1)}, bf16[3,128,640]{2,1,0:T(8,128)(2,1)S(1)}, u32[]{:S(2)}, u32[]{:S(2)}) collective-permute-start(bf16[3,128,640]{2,1,0:T(8,128)(2,1)S(1)} %get-tuple-element.72), channel_id=1, source_target_pairs={{0,2},{1,3},{2,0},{3,1},{4,6},{5,7},{6,4},{7,5},{8,10},{9,11},{10,... | collective-permute-start | bytes 1474568 | tf_op jit(solution)/shard_map/ppermute | solution.py:20
  90.9 34.4 %collective-permute-start.10 = (bf16[512,768]{1,0:T(8,128)(2,1)}, bf16[512,768]{1,0:T(8,128)(2,1)S(1)}, u32[]{:S(2)}, u32[]{:S(2)}) collective-permute-start(bf16[512,768]{1,0:T(8,128)(2,1)} %collective-permute-done.9), channel_id=1, source_target_pairs={{0,4},{4,0},{8,12},{12,8},{16,20},{20,16},{24,28},{28,24},{1,5},{5... | collective-permute-start | bytes 2359304 | tf_op jit(solution)/shard_map/ppermute | solution.py:20
  111.5 50.7 %collective-permute-start.16 = (bf16[640,768]{1,0:T(8,128)(2,1)S(1)}, bf16[640,768]{1,0:T(8,128)(2,1)S(1)}, u32[]{:S(2)}, u32[]{:S(2)}) collective-permute-start(bf16[640,768]{1,0:T(8,128)(2,1)S(1)} %add_convert_fusion.1), channel_id=1, source_target_pairs={{0,16},{4,20},{8,24},{12,28},{16,0},{20,4},{24,8},{28,12},{1,17},{... | collective-permute-start | bytes 2949128 | tf_op jit(solution)/shard_map/ppermute | solution.py:20
  127.7 106.9 %collective-permute-start.13 = (bf16[256,768]{1,0:T(8,128)(2,1)}, bf16[256,768]{1,0:T(8,128)(2,1)}, u32[]{:S(2)}, u32[]{:S(2)}) collective-permute-start(bf16[256,768]{1,0:T(8,128)(2,1)} %slice.376), channel_id=1, source_target_pairs={{0,16},{4,20},{8,24},{12,28},{16,0},{20,4},{24,8},{28,12},{1,17},{... | collective-permute-start | bytes 1179656 | tf_op jit(solution)/shard_map/ppermute | solution.py:20
  129.5 6.7 %collective-permute-start.12 = (bf16[2,3,128,640]{3,2,1,0:T(8,128)(2,1)S(1)}, bf16[2,3,128,640]{3,2,1,0:T(8,128)(2,1)S(1)}, u32[]{:S(2)}, u32[]{:S(2)}) collective-permute-start(bf16[2,3,128,640]{3,2,1,0:T(8,128)(2,1)S(1)} %pad_maximum_fusion.1), channel_id=1, source_target_pairs={{0,1},{1,0},{2,3},{3,2},{4,5},{5,4},{6,7},{7,6},{8,9},{9,8},{10,11... | collective-permute-start | bytes 2949128 | tf_op jit(solution)/shard_map/ppermute | solution.py:20
  131.8 73.7 %collective-permute-start.17 = (bf16[384,1536]{1,0:T(8,128)(2,1)}, bf16[384,1536]{1,0:T(8,128)(2,1)}, u32[]{:S(2)}, u32[]{:S(2)}) collective-permute-start(bf16[384,1536]{1,0:T(8,128)(2,1)} %get-tuple-element.66), channel_id=1, source_target_pairs={{0,4},{4,0},{8,12},{12,8},{16,20},{20,16},{24,28},{28,24},{1,5},{5... | collective-permute-start | bytes 3538952 | tf_op jit(solution)/shard_map/ppermute | solution.py:20
  132.3 70.2 %collective-permute-start.15 = (bf16[384,1536]{1,0:T(8,128)(2,1)}, bf16[384,1536]{1,0:T(8,128)(2,1)}, u32[]{:S(2)}, u32[]{:S(2)}) collective-permute-start(bf16[384,1536]{1,0:T(8,128)(2,1)} %get-tuple-element.66), channel_id=1, source_target_pairs={{0,8},{4,12},{8,0},{12,4},{16,24},{20,28},{24,16},{28,20},{1,9},{5... | collective-permute-start | bytes 3538952 | tf_op jit(solution)/shard_map/ppermute | solution.py:20
  136.3 73.8 %collective-permute-start.18 = (bf16[384,768]{1,0:T(8,128)(2,1)}, bf16[384,768]{1,0:T(8,128)(2,1)}, u32[]{:S(2)}, u32[]{:S(2)}) collective-permute-start(bf16[384,768]{1,0:T(8,128)(2,1)} %slice.386), channel_id=1, source_target_pairs={{0,16},{4,20},{8,24},{12,28},{16,0},{20,4},{24,8},{28,12},{1,17},{... | collective-permute-start | bytes 1769480 | tf_op jit(solution)/shard_map/ppermute | solution.py:20
  202.5 27.8 %collective-permute-start.19 = (bf16[384,1536]{1,0:T(8,128)(2,1)}, bf16[384,1536]{1,0:T(8,128)(2,1)}, u32[]{:S(2)}, u32[]{:S(2)}) collective-permute-start(bf16[384,1536]{1,0:T(8,128)(2,1)} %collective-permute-done.15), channel_id=1, source_target_pairs={{0,4},{4,0},{8,12},{12,8},{16,20},{20,16},{24,28},{28,24},{1,5},{5... | collective-permute-start | bytes 3538952 | tf_op jit(solution)/shard_map/ppermute | solution.py:20
  248.2 7.0 %collective-permute-start.26 = (bf16[8,1,48,256]{3,2,1,0:T(8,128)(2,1)S(1)}, bf16[8,1,48,256]{3,2,1,0:T(8,128)(2,1)S(1)}, u32[]{:S(2)}, u32[]{:S(2)}) collective-permute-start(bf16[8,1,48,256]{3,2,1,0:T(8,128)(2,1)S(1)} %pad_maximum_fusion.10), channel_id=1, source_target_pairs={{0,2},{1,3},{2,0},{3,1},{4,6},{5,7},{6,4},{7,5},{8,10},{9,11},{10,... | collective-permute-start | bytes 589832 | tf_op jit(solution)/shard_map/ppermute | solution.py:20
  255.4 6.3 %collective-permute-start.27 = (bf16[4,48,256]{2,1,0:T(8,128)(2,1)S(1)}, bf16[4,48,256]{2,1,0:T(8,128)(2,1)S(1)}, u32[]{:S(2)}, u32[]{:S(2)}) collective-permute-start(bf16[4,48,256]{2,1,0:T(8,128)(2,1)S(1)} %pad_maximum_fusion.14), channel_id=1, source_target_pairs={{0,16},{4,20},{8,24},{12,28},{16,0},{20,4},{24,8},{28,12},{1,17},{... | collective-permute-start | bytes 294920 | tf_op jit(solution)/shard_map/ppermute | solution.py:20
  255.5 12.4 %collective-permute-start.21 = (bf16[8,1,48,384]{3,2,1,0:T(8,128)(2,1)S(1)}, bf16[8,1,48,384]{3,2,1,0:T(8,128)(2,1)S(1)}, u32[]{:S(2)}, u32[]{:S(2)}) collective-permute-start(bf16[8,1,48,384]{3,2,1,0:T(8,128)(2,1)S(1)} %pad_maximum_fusion.9), channel_id=1, source_target_pairs={{0,2},{1,3},{2,0},{3,1},{4,6},{5,7},{6,4},{7,5},{8,10},{9,11},{10,... | collective-permute-start | bytes 884744 | tf_op jit(solution)/shard_map/ppermute | solution.py:20
  268.2 8.2 %collective-permute-start.22 = (bf16[4,48,384]{2,1,0:T(8,128)(2,1)S(1)}, bf16[4,48,384]{2,1,0:T(8,128)(2,1)S(1)}, u32[]{:S(2)}, u32[]{:S(2)}) collective-permute-start(bf16[4,48,384]{2,1,0:T(8,128)(2,1)S(1)} %pad_maximum_fusion.11), channel_id=1, source_target_pairs={{0,16},{4,20},{8,24},{12,28},{16,0},{20,4},{24,8},{28,12},{1,17},{... | collective-permute-start | bytes 442376 | tf_op jit(solution)/shard_map/ppermute | solution.py:20
  (28 other events, 183.7 us)

commit v3 on v2

--- a/solution.py
+++ b/solution.py
@@ -130,8 +130,10 @@
     return jnp.concatenate([left.reshape(-1, owned, size).astype(jnp.bfloat16) for left in lefts])
 
 
-def exchange_over_dp(blocks, seen, n):
+def exchange_over_dp(blocks, seen, n, direct):
     blocks = {q: blocks[i] for i, q in enumerate(seen)}
+    if direct:
+        return jnp.stack([blocks[0]] + [swap(blocks[q], "dp", q) for q in range(1, n)])
     bit = n // 2
     while bit:
         going = [q for q in range(n) if q & bit]
@@ -229,7 +231,7 @@
     early_other, mark = None, early[-1]
     owned = prompts.shape[0] // n_tensor
     outs = []
-    for start, size in parts:
+    for i, (start, size) in enumerate(parts):
         recvs = [gate(x, mark) for x in received[last, start]]
         *new_state, weight = adam(own_sums[last], recvs, state, new_state, start, last * part_width)
         acc = late_part(most, early, weight, start, size)
@@ -240,7 +242,7 @@
         marks = []
         left = reduce_over_tensor([acc, acc_other], n, owned, t, marks)
         mark = marks[0] if marks else acc_other
-        outs.append(exchange_over_dp(left, seen, n))
+        outs.append(exchange_over_dp(left, seen, n, n <= 8 and i == len(parts) - 1))
     projected = pl.pallas_call(
         functools.partial(place_kernel, rows, [start for start, _ in parts]),
         in_specs=[pl.BlockSpec(memory_space=pltpu.SMEM)] + [pl.BlockSpec(memory_space=pltpu.VMEM)] * len(outs),

time: 291 us -> 296 us (1.017)
  starting transfers between devices: 31.1 us -> 39.3 us
    ppermute x30 -> x34, starting transfers between devices: 31.1 us -> 39.3 us  [swap(): return lax.ppermute(x, axis, [(i, i ^ bit) for i in range(n)])]
    ppermute x30 -> x34, waiting for transfers between devices: 171 us -> 169 us  [swap(): return lax.ppermute(x, axis, [(i, i ^ bit) for i in range(n)])]
  transfers between devices with their start and end apart: 30 -> 34, of which waited for: 18 -> 17; matrix products, arithmetic and copies ran while one was open for 18% -> 18% of each run, Pallas kernels for 5% -> 5%
where the time goes in v3:
time: 296 us; the launch traced here: 295 us
  waiting for transfers between devices  169 us (57%)
  starting transfers between devices  39.3 us (13%)
  matrix products  36.7 us (12%)
  local copies, waits for them, and re-layouts  24 us (8%)
  Pallas kernels  19 us (6%)
  other arithmetic  5.92 us (2%)
    ppermute x34, waiting for transfers between devices, swap(): return lax.ppermute(x, axis, [(i, i ^ bit) for i in range(n)])  169 us
    ppermute x34, starting transfers between devices, swap(): return lax.ppermute(x, axis, [(i, i ^ bit) for i in range(n)])  39.3 us
    dot_general x16, matrix products, dot_tokens(): lax.dot_general(cot, acts, (((0,), (0,)), ((), ())), preferred_element_ty...  22.3 us
    pallas_call x3, Pallas kernels, adam(): pl.pallas_call(functools.partial(adam_kernel, len(recvs)), grid=(rows //...  17.1 us
    dot_general x6, matrix products, dot_features(): lax.dot_general(rows, weight, (((1,), (1,)), ((), ())), preferred_element...  14.3 us
    unnamed x60, local copies, waits for them, and re-layouts  8.63 us
  transfers between devices with their start and end apart: 34, of which 17 were waited for; matrix products, arithmetic and copies ran while one was open for 18% of the time, Pallas kernels for 5%

profile of v3, /device:TPU:0, one launch (start us, length us, event | category | flops | bytes accessed | tf_op | source)
XLA Modules:
  0.0 295.1 jit_solution(8306286472045820041)
XLA Ops:
  2.2 4.1 %collective-permute-start.2 = (bf16[128,1280]{1,0:T(8,128)(2,1)S(1)}, bf16[128,1280]{1,0:T(8,128)(2,1)S(1)}, u32[]{:S(2)}, u32[]{:S(2)}) collective-permute-start(bf16[128,1280]{1,0:T(8,128)(2,1)S(1)} %pad_maximum_fusion.8), channel_id=1, source_target_pairs={{0,12},{4,8},{8,4},{12,0},{16,28},{20,24},{24,20},{28,16},{1,13},{... | collective-permute-start | bytes 983048 | tf_op jit(solution)/shard_map/ppermute | solution.py:20
  7.0 7.8 %collective-permute-done.2 = bf16[128,1280]{1,0:T(8,128)(2,1)S(1)} collective-permute-done((bf16[128,1280]{1,0:T(8,128)(2,1)S(1)}, bf16[128,1280]{1,0:T(8,128)(2,1)S(1)}, u32[]{:S(2)}, u32[]{:S(2)}) %collective-permute-start.2) | collective-permute-done | bytes 327712 | tf_op jit(solution)/shard_map/ppermute | solution.py:20
  15.5 5.6 %collective-permute-done.1 = bf16[128,1280]{1,0:T(8,128)(2,1)S(1)} collective-permute-done((bf16[128,1280]{1,0:T(8,128)(2,1)S(1)}, bf16[128,1280]{1,0:T(8,128)(2,1)S(1)}, u32[]{:S(2)}, u32[]{:S(2)}) %collective-permute-start.1) | collective-permute-done | bytes 327712 | tf_op jit(solution)/shard_map/ppermute | solution.py:20
  24.5 10.7 %collective-permute-done.3 = bf16[3,128,640]{2,1,0:T(8,128)(2,1)S(1)} collective-permute-done((bf16[3,128,640]{2,1,0:T(8,128)(2,1)S(1)}, bf16[3,128,640]{2,1,0:T(8,128)(2,1)S(1)}, u32[]{:S(2)}, u32[]{:S(2)}) %collective-permute-start.3) | collective-permute-done | bytes 491552 | tf_op jit(solution)/shard_map/ppermute | solution.py:20
  41.5 2.6 collective-permute-start.14
  53.1 20.2 %collective-permute-done.6 = bf16[512,768]{1,0:T(8,128)(2,1)} collective-permute-done((bf16[512,768]{1,0:T(8,128)(2,1)}, bf16[512,768]{1,0:T(8,128)(2,1)}, u32[]{:S(2)}, u32[]{:S(2)}) %collective-permute-start.6) | collective-permute-done | bytes 786464 | tf_op jit(solution)/shard_map/ppermute | solution.py:20
  77.7 11.7 %collective-permute-done.9 = bf16[512,768]{1,0:T(8,128)(2,1)} collective-permute-done((bf16[512,768]{1,0:T(8,128)(2,1)}, bf16[512,768]{1,0:T(8,128)(2,1)}, u32[]{:S(2)}, u32[]{:S(2)}) %collective-permute-start.9) | collective-permute-done | bytes 786464 | tf_op jit(solution)/shard_map/ppermute | solution.py:20
  95.1 15.6 %collective-permute-done.7 = bf16[512,768]{1,0:T(8,128)(2,1)S(1)} collective-permute-done((bf16[512,768]{1,0:T(8,128)(2,1)}, bf16[512,768]{1,0:T(8,128)(2,1)S(1)}, u32[]{:S(2)}, u32[]{:S(2)}) %collective-permute-start.7) | collective-permute-done | bytes 786464 | tf_op jit(solution)/shard_map/ppermute | solution.py:20
  116.6 8.7 %collective-permute-done.10 = bf16[512,768]{1,0:T(8,128)(2,1)S(1)} collective-permute-done((bf16[512,768]{1,0:T(8,128)(2,1)}, bf16[512,768]{1,0:T(8,128)(2,1)S(1)}, u32[]{:S(2)}, u32[]{:S(2)}) %collective-permute-start.10) | collective-permute-done | bytes 786464 | tf_op jit(solution)/shard_map/ppermute | solution.py:20
  132.3 2.5 collective-permute-start.15
  145.0 17.2 %collective-permute-done.16.refs_1_ = bf16[640,768]{1,0:T(8,128)(2,1)S(1)} collective-permute-done((bf16[640,768]{1,0:T(8,128)(2,1)S(1)}, bf16[640,768]{1,0:T(8,128)(2,1)S(1)}, u32[]{:S(2)}, u32[]{:S(2)}) %collective-permute-start.16) | collective-permute-done | bytes 983072 | tf_op jit(solution)/shard_map/ppermute | solution.py:20
  165.2 8.5 %adam.3 = (f32[640,1536]{1,0:T(8,128)}, f32[640,1536]{1,0:T(8,128)}, f32[640,1536]{1,0:T(8,128)}, bf16[640,768]{1,0:T(8,128)(2,1)}) custom-call(f32[640,768]{1,0:T(8,128)} %convolution_add_fusion.2.refs_0_, bf16[640,768]{1,0:T(8,128)(2,1)} %copy-done.14, f32[640,1536]{1,0:T(8,128)} %refs_2_.5, f32[640,1536]{1,0:T(8,128)} %refs_3_.5, f32[640,1536]{1,0:T(8,128)} %refs_4_.5), custom_call_target="tpu_custom_call" | custom-call | flops 9830400 | bytes 15728640 | tf_op jit(solution)/shard_map/adam/pallas_call | solution.py:66
  173.7 28.8 %collective-permute-done.15 = bf16[384,1536]{1,0:T(8,128)(2,1)} collective-permute-done((bf16[384,1536]{1,0:T(8,128)(2,1)}, bf16[384,1536]{1,0:T(8,128)(2,1)}, u32[]{:S(2)}, u32[]{:S(2)}) %collective-permute-start.15) | collective-permute-done | bytes 1179680 | tf_op jit(solution)/shard_map/ppermute | solution.py:20
  206.8 3.2 %fusion = f32[1152,640]{1,0:T(8,128)} fusion(bf16[640,768]{1,0:T(8,128)(2,1)S(1)} %copy-done.15, bf16[1152,1536]{1,0:T(8,128)(2,1)S(1)} %constant_dynamic-update-slice_fusion.2), kind=kOutput, calls=%fused_computation.8 | convolution fusion | flops 1132462080 | bytes 5701632 | tf_op jit(solution)/shard_map/dot_general | solution.py:28
  210.0 5.4 %adam.4 = (f32[640,1536]{1,0:T(8,128)}, f32[640,1536]{1,0:T(8,128)}, f32[640,1536]{1,0:T(8,128)}, bf16[384,768]{1,0:T(8,128)(2,1)}) custom-call(f32[640,768]{1,0:T(8,128)} %convolution_add_fusion.3.refs_0_, bf16[384,768]{1,0:T(8,128)(2,1)} %collective-permute-done.18.refs_1_, ...), custom_call_target="tpu_custom_call", output_to_operand_aliasing={{0}: (5, {}), {1}: (6, {}), {2}: (7, {})} | custom-call | flops 5898240 | bytes 9437184 | tf_op jit(solution)/shard_map/adam/pallas_call | solution.py:66
  215.4 3.4 %convolution_add_fusion = f32[1152,384]{1,0:T(8,128)S(1)} fusion(bf16[384,768]{1,0:T(8,128)(2,1)} %get-tuple-element.46, f32[1152,640]{1,0:T(8,128)} %fusion, bf16[1152,1536]{1,0:T(8,128)(2,1)} %copy-done.6), kind=kOutput, calls=%fused_computation | convolution fusion | flops 679919616 | bytes 5898240 | tf_op jit(solution)/shard_map/dot_general | solution.py:28
  218.8 11.5 %collective-permute-done.19 = bf16[384,1536]{1,0:T(8,128)(2,1)} collective-permute-done((bf16[384,1536]{1,0:T(8,128)(2,1)}, bf16[384,1536]{1,0:T(8,128)(2,1)}, u32[]{:S(2)}, u32[]{:S(2)}) %collective-permute-start.19) | collective-permute-done | bytes 1179680 | tf_op jit(solution)/shard_map/ppermute | solution.py:20
  234.6 3.3 %adam.5 = (f32[640,1536]{1,0:T(8,128)}, f32[640,1536]{1,0:T(8,128)}, f32[640,1536]{1,0:T(8,128)}, bf16[256,768]{1,0:T(8,128)(2,1)}) custom-call(f32[640,768]{1,0:T(8,128)} %convolution_add_fusion.3.refs_0_, bf16[256,768]{1,0:T(8,128)(2,1)} %collective-permute-done.13.refs_1_, ...), custom_call_target="tpu_custom_call", output_to_operand_aliasing={{0}: (5, {}), {1}: (6, {}), {2}: (7, {})} | custom-call | flops 3932160 | bytes 6291456 | tf_op jit(solution)/shard_map/adam/pallas_call | solution.py:66
  237.8 2.6 convolution_add_fusion.1
  250.7 5.3 %collective-permute-done.26 = bf16[8,1,48,256]{3,2,1,0:T(8,128)(2,1)S(1)} collective-permute-done((bf16[8,1,48,256]{3,2,1,0:T(8,128)(2,1)S(1)}, bf16[8,1,48,256]{3,2,1,0:T(8,128)(2,1)S(1)}, u32[]{:S(2)}, u32[]{:S(2)}) %collective-permute-start.26) | collective-permute-done | bytes 196640 | tf_op jit(solution)/shard_map/ppermute | solution.py:20
  269.3 5.1 %collective-permute-done.30 = bf16[48,256]{1,0:T(8,128)(2,1)S(1)} collective-permute-done((bf16[48,256]{1,0:T(8,128)(2,1)S(1)}, bf16[48,256]{1,0:T(8,128)(2,1)S(1)}, u32[]{:S(2)}, u32[]{:S(2)}) %collective-permute-start.30) | collective-permute-done | bytes 24608 | tf_op jit(solution)/shard_map/ppermute | solution.py:20
  274.7 7.2 %collective-permute-done.22 = bf16[4,48,384]{2,1,0:T(8,128)(2,1)S(1)} collective-permute-done((bf16[4,48,384]{2,1,0:T(8,128)(2,1)S(1)}, bf16[4,48,384]{2,1,0:T(8,128)(2,1)S(1)}, u32[]{:S(2)}, u32[]{:S(2)}) %collective-permute-start.22) | collective-permute-done | bytes 147488 | tf_op jit(solution)/shard_map/ppermute | solution.py:20
  282.1 5.1 %collective-permute-done.23 = bf16[4,48,384]{2,1,0:T(8,128)(2,1)S(1)} collective-permute-done((bf16[4,48,384]{2,1,0:T(8,128)(2,1)S(1)}, bf16[4,48,384]{2,1,0:T(8,128)(2,1)S(1)}, u32[]{:S(2)}, u32[]{:S(2)}) %collective-permute-start.23) | collective-permute-done | bytes 147488 | tf_op jit(solution)/shard_map/ppermute | solution.py:20
  287.8 4.6 %collective-permute-done.24 = bf16[4,48,384]{2,1,0:T(8,128)(2,1)S(1)} collective-permute-done((bf16[4,48,384]{2,1,0:T(8,128)(2,1)S(1)}, bf16[4,48,384]{2,1,0:T(8,128)(2,1)S(1)}, u32[]{:S(2)}, u32[]{:S(2)}) %collective-permute-start.24) | collective-permute-done | bytes 147488 | tf_op jit(solution)/shard_map/ppermute | solution.py:20
  (190 shorter events, 92.9 us)
Async XLA Ops:
  2.2 12.7 %collective-permute-start.2 = (bf16[128,1280]{1,0:T(8,128)(2,1)S(1)}, bf16[128,1280]{1,0:T(8,128)(2,1)S(1)}, u32[]{:S(2)}, u32[]{:S(2)}) collective-permute-start(bf16[128,1280]{1,0:T(8,128)(2,1)S(1)} %pad_maximum_fusion.8), channel_id=1, source_target_pairs={{0,12},{4,8},{8,4},{12,0},{16,28},{20,24},{24,20},{28,16},{1,13},{... | collective-permute-start | bytes 983048 | tf_op jit(solution)/shard_map/ppermute | solution.py:20
  6.3 14.9 %collective-permute-start.1 = (bf16[128,1280]{1,0:T(8,128)(2,1)S(1)}, bf16[128,1280]{1,0:T(8,128)(2,1)S(1)}, u32[]{:S(2)}, u32[]{:S(2)}) collective-permute-start(bf16[128,1280]{1,0:T(8,128)(2,1)S(1)} %pad_maximum_fusion.7), channel_id=1, source_target_pairs={{0,8},{4,12},{8,0},{12,4},{16,24},{20,28},{24,16},{28,20},{1,9},{5... | collective-permute-start | bytes 983048 | tf_op jit(solution)/shard_map/ppermute | solution.py:20
  6.8 15.1 %collective-permute-start = (bf16[128,1280]{1,0:T(8,128)(2,1)S(1)}, bf16[128,1280]{1,0:T(8,128)(2,1)S(1)}, u32[]{:S(2)}, u32[]{:S(2)}) collective-permute-start(bf16[128,1280]{1,0:T(8,128)(2,1)S(1)} %pad_maximum_fusion.6), channel_id=1, source_target_pairs={{0,4},{4,0},{8,12},{12,8},{16,20},{20,16},{24,28},{28,24},{1,5},{5... | collective-permute-start | bytes 983048 | tf_op jit(solution)/shard_map/ppermute | solution.py:20
  22.9 12.3 %collective-permute-start.3 = (bf16[3,128,640]{2,1,0:T(8,128)(2,1)S(1)}, bf16[3,128,640]{2,1,0:T(8,128)(2,1)S(1)}, u32[]{:S(2)}, u32[]{:S(2)}) collective-permute-start(bf16[3,128,640]{2,1,0:T(8,128)(2,1)S(1)} %get-tuple-element.75), channel_id=1, source_target_pairs={{0,2},{1,3},{2,0},{3,1},{4,6},{5,7},{6,4},{7,5},{8,10},{9,11},{10,... | collective-permute-start | bytes 1474568 | tf_op jit(solution)/shard_map/ppermute | solution.py:20
  37.1 36.6 %collective-permute-start.4 = (bf16[2,3,128,640]{3,2,1,0:T(8,128)(2,1)}, bf16[2,3,128,640]{3,2,1,0:T(8,128)(2,1)}, u32[]{:S(2)}, u32[]{:S(2)}) collective-permute-start(bf16[2,3,128,640]{3,2,1,0:T(8,128)(2,1)} %pad_maximum_fusion), channel_id=1, source_target_pairs={{0,1},{1,0},{2,3},{3,2},{4,5},{5,4},{6,7},{7,6},{8,9},{9,8},{10,11... | collective-permute-start | bytes 2949128 | tf_op jit(solution)/shard_map/ppermute | solution.py:20
  38.3 52.6 %collective-permute-start.5 = (bf16[512,768]{1,0:T(8,128)(2,1)}, bf16[512,768]{1,0:T(8,128)(2,1)}, u32[]{:S(2)}, u32[]{:S(2)}) collective-permute-start(bf16[512,768]{1,0:T(8,128)(2,1)} %get-tuple-element.65), channel_id=1, source_target_pairs={{0,4},{4,0},{8,12},{12,8},{16,20},{20,16},{24,28},{28,24},{1,5},{5... | collective-permute-start | bytes 2359304 | tf_op jit(solution)/shard_map/ppermute | solution.py:20
  39.9 33.4 %collective-permute-start.6 = (bf16[512,768]{1,0:T(8,128)(2,1)}, bf16[512,768]{1,0:T(8,128)(2,1)}, u32[]{:S(2)}, u32[]{:S(2)}) collective-permute-start(bf16[512,768]{1,0:T(8,128)(2,1)} %get-tuple-element.65), channel_id=1, source_target_pairs={{0,8},{4,12},{8,0},{12,4},{16,24},{20,28},{24,16},{28,20},{1,9},{5... | collective-permute-start | bytes 2359304 | tf_op jit(solution)/shard_map/ppermute | solution.py:20
  41.5 87.9 %collective-permute-start.14 = (bf16[192,1536]{1,0:T(8,128)(2,1)}, bf16[192,1536]{1,0:T(8,128)(2,1)}, u32[]{:S(2)}, u32[]{:S(2)}) collective-permute-start(bf16[192,1536]{1,0:T(8,128)(2,1)} %param.11), channel_id=1, source_target_pairs={{0,16},{4,20},{8,24},{12,28},{16,0},{20,4},{24,8},{28,12},{1,17},{... | collective-permute-start | bytes 1769480 | tf_op jit(solution)/shard_map/ppermute | solution.py:20
  44.1 45.3 %collective-permute-start.9 = (bf16[512,768]{1,0:T(8,128)(2,1)}, bf16[512,768]{1,0:T(8,128)(2,1)}, u32[]{:S(2)}, u32[]{:S(2)}) collective-permute-start(bf16[512,768]{1,0:T(8,128)(2,1)} %get-tuple-element.64), channel_id=1, source_target_pairs={{0,8},{4,12},{8,0},{12,4},{16,24},{20,28},{24,16},{28,20},{1,9},{5... | collective-permute-start | bytes 2359304 | tf_op jit(solution)/shard_map/ppermute | solution.py:20
  73.3 40.7 %collective-permute-start.8 = (bf16[512,768]{1,0:T(8,128)(2,1)}, bf16[512,768]{1,0:T(8,128)(2,1)S(1)}, u32[]{:S(2)}, u32[]{:S(2)}) collective-permute-start(bf16[512,768]{1,0:T(8,128)(2,1)} %get-tuple-element.64), channel_id=1, source_target_pairs={{0,4},{4,0},{8,12},{12,8},{16,20},{20,16},{24,28},{28,24},{1,5},{5... | collective-permute-start | bytes 2359304 | tf_op jit(solution)/shard_map/ppermute | solution.py:20
  73.7 37.1 %collective-permute-start.7 = (bf16[512,768]{1,0:T(8,128)(2,1)}, bf16[512,768]{1,0:T(8,128)(2,1)S(1)}, u32[]{:S(2)}, u32[]{:S(2)}) collective-permute-start(bf16[512,768]{1,0:T(8,128)(2,1)} %collective-permute-done.6), channel_id=1, source_target_pairs={{0,4},{4,0},{8,12},{12,8},{16,20},{20,16},{24,28},{28,24},{1,5},{5... | collective-permute-start | bytes 2359304 | tf_op jit(solution)/shard_map/ppermute | solution.py:20
  89.4 40.0 %collective-permute-start.11 = (bf16[3,128,640]{2,1,0:T(8,128)(2,1)S(1)}, bf16[3,128,640]{2,1,0:T(8,128)(2,1)S(1)}, u32[]{:S(2)}, u32[]{:S(2)}) collective-permute-start(bf16[3,128,640]{2,1,0:T(8,128)(2,1)S(1)} %get-tuple-element.72), channel_id=1, source_target_pairs={{0,2},{1,3},{2,0},{3,1},{4,6},{5,7},{6,4},{7,5},{8,10},{9,11},{10,... | collective-permute-start | bytes 1474568 | tf_op jit(solution)/shard_map/ppermute | solution.py:20
  90.9 34.4 %collective-permute-start.10 = (bf16[512,768]{1,0:T(8,128)(2,1)}, bf16[512,768]{1,0:T(8,128)(2,1)S(1)}, u32[]{:S(2)}, u32[]{:S(2)}) collective-permute-start(bf16[512,768]{1,0:T(8,128)(2,1)} %collective-permute-done.9), channel_id=1, source_target_pairs={{0,4},{4,0},{8,12},{12,8},{16,20},{20,16},{24,28},{28,24},{1,5},{5... | collective-permute-start | bytes 2359304 | tf_op jit(solution)/shard_map/ppermute | solution.py:20
  111.5 50.7 %collective-permute-start.16 = (bf16[640,768]{1,0:T(8,128)(2,1)S(1)}, bf16[640,768]{1,0:T(8,128)(2,1)S(1)}, u32[]{:S(2)}, u32[]{:S(2)}) collective-permute-start(bf16[640,768]{1,0:T(8,128)(2,1)S(1)} %add_convert_fusion.1), channel_id=1, source_target_pairs={{0,16},{4,20},{8,24},{12,28},{16,0},{20,4},{24,8},{28,12},{1,17},{... | collective-permute-start | bytes 2949128 | tf_op jit(solution)/shard_map/ppermute | solution.py:20
  127.7 106.9 %collective-permute-start.13 = (bf16[256,768]{1,0:T(8,128)(2,1)}, bf16[256,768]{1,0:T(8,128)(2,1)}, u32[]{:S(2)}, u32[]{:S(2)}) collective-permute-start(bf16[256,768]{1,0:T(8,128)(2,1)} %slice.309), channel_id=1, source_target_pairs={{0,16},{4,20},{8,24},{12,28},{16,0},{20,4},{24,8},{28,12},{1,17},{... | collective-permute-start | bytes 1179656 | tf_op jit(solution)/shard_map/ppermute | solution.py:20
  131.8 73.6 %collective-permute-start.17 = (bf16[384,1536]{1,0:T(8,128)(2,1)}, bf16[384,1536]{1,0:T(8,128)(2,1)}, u32[]{:S(2)}, u32[]{:S(2)}) collective-permute-start(bf16[384,1536]{1,0:T(8,128)(2,1)} %get-tuple-element.66), channel_id=1, source_target_pairs={{0,4},{4,0},{8,12},{12,8},{16,20},{20,16},{24,28},{28,24},{1,5},{5... | collective-permute-start | bytes 3538952 | tf_op jit(solution)/shard_map/ppermute | solution.py:20
  132.3 70.2 %collective-permute-start.15 = (bf16[384,1536]{1,0:T(8,128)(2,1)}, bf16[384,1536]{1,0:T(8,128)(2,1)}, u32[]{:S(2)}, u32[]{:S(2)}) collective-permute-start(bf16[384,1536]{1,0:T(8,128)(2,1)} %get-tuple-element.66), channel_id=1, source_target_pairs={{0,8},{4,12},{8,0},{12,4},{16,24},{20,28},{24,16},{28,20},{1,9},{5... | collective-permute-start | bytes 3538952 | tf_op jit(solution)/shard_map/ppermute | solution.py:20
  136.2 73.7 %collective-permute-start.18 = (bf16[384,768]{1,0:T(8,128)(2,1)}, bf16[384,768]{1,0:T(8,128)(2,1)}, u32[]{:S(2)}, u32[]{:S(2)}) collective-permute-start(bf16[384,768]{1,0:T(8,128)(2,1)} %slice.319), channel_id=1, source_target_pairs={{0,16},{4,20},{8,24},{12,28},{16,0},{20,4},{24,8},{28,12},{1,17},{... | collective-permute-start | bytes 1769480 | tf_op jit(solution)/shard_map/ppermute | solution.py:20
  202.5 27.8 %collective-permute-start.19 = (bf16[384,1536]{1,0:T(8,128)(2,1)}, bf16[384,1536]{1,0:T(8,128)(2,1)}, u32[]{:S(2)}, u32[]{:S(2)}) collective-permute-start(bf16[384,1536]{1,0:T(8,128)(2,1)} %collective-permute-done.15), channel_id=1, source_target_pairs={{0,4},{4,0},{8,12},{12,8},{16,20},{20,16},{24,28},{28,24},{1,5},{5... | collective-permute-start | bytes 3538952 | tf_op jit(solution)/shard_map/ppermute | solution.py:20
  250.1 24.3 %collective-permute-start.21 = (bf16[8,1,48,384]{3,2,1,0:T(8,128)(2,1)S(1)}, bf16[8,1,48,384]{3,2,1,0:T(8,128)(2,1)S(1)}, u32[]{:S(2)}, u32[]{:S(2)}) collective-permute-start(bf16[8,1,48,384]{3,2,1,0:T(8,128)(2,1)S(1)} %pad_maximum_fusion.9), channel_id=1, source_target_pairs={{0,2},{1,3},{2,0},{3,1},{4,6},{5,7},{6,4},{7,5},{8,10},{9,11},{10,... | collective-permute-start | bytes 884744 | tf_op jit(solution)/shard_map/ppermute | solution.py:20
  257.7 24.4 %collective-permute-start.33 = (bf16[48,256]{1,0:T(8,128)(2,1)S(1)}, bf16[48,256]{1,0:T(8,128)(2,1)S(1)}, u32[]{:S(2)}, u32[]{:S(2)}) collective-permute-start(bf16[48,256]{1,0:T(8,128)(2,1)S(1)} %get-tuple-element.96), channel_id=1, source_target_pairs={{0,28},{4,24},{8,20},{12,16},{16,12},{20,8},{24,4},{28,0},{1,29},{... | collective-permute-start | bytes 73736 | tf_op jit(solution)/shard_map/ppermute | solution.py:20
  259.5 8.2 %collective-permute-start.29 = (bf16[48,256]{1,0:T(8,128)(2,1)S(1)}, bf16[48,256]{1,0:T(8,128)(2,1)S(1)}, u32[]{:S(2)}, u32[]{:S(2)}) collective-permute-start(bf16[48,256]{1,0:T(8,128)(2,1)S(1)} %get-tuple-element.97), channel_id=1, source_target_pairs={{0,12},{4,8},{8,4},{12,0},{16,28},{20,24},{24,20},{28,16},{1,13},{... | collective-permute-start | bytes 73736 | tf_op jit(solution)/shard_map/ppermute | solution.py:20
  259.5 15.2 %collective-permute-start.32 = (bf16[48,256]{1,0:T(8,128)(2,1)S(1)}, bf16[48,256]{1,0:T(8,128)(2,1)S(1)}, u32[]{:S(2)}, u32[]{:S(2)}) collective-permute-start(bf16[48,256]{1,0:T(8,128)(2,1)S(1)} %get-tuple-element.87), channel_id=1, source_target_pairs={{0,24},{4,28},{8,16},{12,20},{16,8},{20,12},{24,0},{28,4},{1,25},{... | collective-permute-start | bytes 73736 | tf_op jit(solution)/shard_map/ppermute | solution.py:20
  265.4 8.9 %collective-permute-start.31 = (bf16[48,256]{1,0:T(8,128)(2,1)S(1)}, bf16[48,256]{1,0:T(8,128)(2,1)S(1)}, u32[]{:S(2)}, u32[]{:S(2)}) collective-permute-start(bf16[48,256]{1,0:T(8,128)(2,1)S(1)} %get-tuple-element.88), channel_id=1, source_target_pairs={{0,20},{4,16},{8,28},{12,24},{16,4},{20,0},{24,12},{28,8},{1,21},{... | collective-permute-start | bytes 73736 | tf_op jit(solution)/shard_map/ppermute | solution.py:20
  (32 other events, 217.5 us)
